TPU v7x, 32 devices: a whole 2x2x4 slice. The times are simulated.
32 devices in a mesh: dp: 8 (over z, x), mp: 4 (over y, core).
Axes of the slice: x: 2, y: 2, z: 4, core: 2. Of those that a mesh axis runs over, the one named last changes fastest.
Arguments:
- tokens: bfloat16 [16384, 1024], P('dp'), may hold values from -6 to 6
- segment_ids: int32 [8, 2048], P('dp'), may hold values from 0 to 127, never falling along the last dimension, each value on 1 to 512 neighbouring positions
- w_query: bfloat16 [1024, 1024], P(None, 'mp'), may hold values from -0.1875 to 0.1875
- w_key: bfloat16 [1024, 1024], P(None, 'mp'), may hold values from -0.1875 to 0.1875
- w_value: bfloat16 [1024, 1024], P(None, 'mp'), may hold values from -0.1875 to 0.1875
- w_gate: bfloat16 [1024, 1024], P(None, 'mp'), may hold values from -0.1875 to 0.1875
- w_out: bfloat16 [1024, 1024], P('mp'), may hold values from -0.25 to 0.25
- w_left: bfloat16 [1024, 2816], P(None, 'mp'), may hold values from -0.1875 to 0.1875
- w_right: bfloat16 [1024, 2816], P(None, 'mp'), may hold values from -0.1875 to 0.1875
- w_down: bfloat16 [2816, 1024], P('mp'), may hold values from -0.109375 to 0.109375
- cotangent: bfloat16 [16384, 1024], P('dp'), may hold values from -6 to 6
Outputs:
- output: bfloat16 [16384, 1024], P('dp')
- grad_tokens: bfloat16 [16384, 1024], P('dp')
- grad_w_query: float32 [1024, 1024], P('dp', 'mp')
- grad_w_key: float32 [1024, 1024], P('dp', 'mp')
- grad_w_value: float32 [1024, 1024], P('dp', 'mp')
- grad_w_gate: float32 [1024, 1024], P('dp', 'mp')
- grad_w_out: float32 [1024, 1024], P('mp', 'dp')
- grad_w_left: float32 [1024, 2816], P('dp', 'mp')
- grad_w_right: float32 [1024, 2816], P('dp', 'mp')
- grad_w_down: float32 [2816, 1024], P('mp', 'dp')
Inputs may be any that keep to these rules, and one draw needn't show every extreme that they name: `segment_ids`: in each row of 2048 positions the ids never fall; a document spans 1 to 512 positions, and one of them exactly that many.
All inputs are finite; a program needn't handle non-finite values.
Results may differ from a plain program's by a relative error of at most 0.02.
Values may be sent and summed in bfloat16 or wider, within the bound.
A program may use at most 192 MiB of HBM per device.

v0:
```python
import jax
import jax.numpy as jnp
from jax import lax
from jax.sharding import PartitionSpec as P

HD = 64
BLOCK = 64


def head_total(partial_value):
    return lax.psum(partial_value.astype(jnp.bfloat16), "mp").astype(jnp.float32)


def rms_factor(values):
    return lax.rsqrt(jnp.mean(values * values, axis=-1, keepdims=True) + 1e-06)


def norm_back(grad, normed, factor):
    return factor * (grad - normed * jnp.mean(grad * normed, axis=-1, keepdims=True))


def block_scores(query_blocks, key_blocks, allowed):
    scores = jnp.einsum(
        "bqhd,bkhd->bhqk", query_blocks, key_blocks, preferred_element_type=jnp.float32
    ) * HD ** (-0.5)
    return jnp.where(allowed[:, None], scores, jnp.float32(-1e30))


def body(
    tokens, segment_ids, w_query, w_key, w_value, w_gate, w_out, w_left, w_right, w_down, cotangent
):
    rows_all = tokens.shape[0]
    width_c = w_query.shape[1]
    heads_here = width_c // HD
    blocks = rows_all // BLOCK
    source = tokens.astype(jnp.float32)
    recip_one = rms_factor(source)
    normed_one = source * recip_one
    normed_low = normed_one.astype(jnp.bfloat16)
    queries = jnp.dot(normed_low, w_query, preferred_element_type=jnp.float32).astype(jnp.bfloat16)
    keys_all = jnp.dot(normed_low, w_key, preferred_element_type=jnp.float32).astype(jnp.bfloat16)
    values_all = jnp.dot(normed_low, w_value, preferred_element_type=jnp.float32).astype(
        jnp.bfloat16
    )
    gate_pre = jnp.dot(normed_low, w_gate, preferred_element_type=jnp.float32).reshape(
        rows_all, heads_here, HD
    )
    query_blocks = queries.reshape(blocks, BLOCK, heads_here, HD)
    key_blocks = keys_all.reshape(blocks, BLOCK, heads_here, HD)
    value_blocks = values_all.reshape(blocks, BLOCK, heads_here, HD)
    seg_blocks = segment_ids.reshape(blocks, BLOCK)
    lower = jnp.arange(BLOCK)[:, None] >= jnp.arange(BLOCK)[None, :]
    allowed = (seg_blocks[:, :, None] == seg_blocks[:, None, :]) & lower[None]
    masked = block_scores(query_blocks, key_blocks, allowed)
    top = jnp.max(masked, axis=-1, keepdims=True)
    expd = jnp.exp(masked - top)
    total = jnp.sum(expd, axis=-1, keepdims=True)
    log_total = top + jnp.log(total)
    probs_low = (expd / total).astype(jnp.bfloat16)
    attended = jnp.einsum(
        "bhqk,bkhd->bqhd", probs_low, value_blocks, preferred_element_type=jnp.float32
    )
    attended = attended.reshape(rows_all, heads_here, HD)
    head_factor = rms_factor(attended)
    head_normed = attended * head_factor
    sigma = jax.nn.sigmoid(gate_pre)
    gated = (head_normed * sigma).reshape(rows_all, width_c).astype(jnp.bfloat16)
    attn_sum = head_total(jnp.dot(gated, w_out, preferred_element_type=jnp.float32))
    hidden = source + attn_sum
    recip_two = rms_factor(hidden)
    normed_two = hidden * recip_two
    normed_two_low = normed_two.astype(jnp.bfloat16)
    left = jnp.dot(normed_two_low, w_left, preferred_element_type=jnp.float32)
    right = jnp.dot(normed_two_low, w_right, preferred_element_type=jnp.float32)
    mixed = (left * right).astype(jnp.bfloat16)
    glu_sum = head_total(jnp.dot(mixed, w_down, preferred_element_type=jnp.float32))
    output = (hidden + glu_sum).astype(jnp.bfloat16)
    grad_down = jnp.einsum("tf,tc->fc", mixed, cotangent, preferred_element_type=jnp.float32)
    d_mixed = jnp.einsum("tc,fc->tf", cotangent, w_down, preferred_element_type=jnp.float32)
    d_left = (d_mixed * right).astype(jnp.bfloat16)
    d_right = (d_mixed * left).astype(jnp.bfloat16)
    grad_left = jnp.einsum("td,tf->df", normed_two_low, d_left, preferred_element_type=jnp.float32)
    grad_right = jnp.einsum(
        "td,tf->df", normed_two_low, d_right, preferred_element_type=jnp.float32
    )
    glu_grads = (
        lax.psum_scatter(grad_left, "dp", scatter_dimension=0, tiled=True),
        lax.psum_scatter(grad_right, "dp", scatter_dimension=0, tiled=True),
        lax.psum_scatter(grad_down, "dp", scatter_dimension=1, tiled=True),
    )
    d_partial_two = jnp.einsum("tf,df->td", d_left, w_left, preferred_element_type=jnp.float32)
    d_partial_two = d_partial_two + jnp.einsum(
        "tf,df->td", d_right, w_right, preferred_element_type=jnp.float32
    )
    d_norm_two = head_total(d_partial_two)
    d_hidden = cotangent.astype(jnp.float32) + norm_back(d_norm_two, normed_two, recip_two)
    d_out_low = d_hidden.astype(jnp.bfloat16)
    grad_out = jnp.einsum("tc,td->cd", gated, d_out_low, preferred_element_type=jnp.float32)
    d_gated = jnp.einsum("td,cd->tc", d_out_low, w_out, preferred_element_type=jnp.float32)
    d_gated = d_gated.reshape(rows_all, heads_here, HD)
    d_head = d_gated * sigma
    d_gate = (
        (d_gated * head_normed * sigma * (1.0 - sigma))
        .reshape(rows_all, width_c)
        .astype(jnp.bfloat16)
    )
    d_attended = norm_back(d_head, head_normed, head_factor).astype(jnp.bfloat16)
    d_attended = d_attended.reshape(blocks, BLOCK, heads_here, HD)
    probs = jnp.exp(block_scores(query_blocks, key_blocks, allowed) - log_total)
    probs_back = probs.astype(jnp.bfloat16)
    d_probs = jnp.einsum(
        "bqhd,bkhd->bhqk", d_attended, value_blocks, preferred_element_type=jnp.float32
    )
    d_values = jnp.einsum(
        "bhqk,bqhd->bkhd", probs_back, d_attended, preferred_element_type=jnp.float32
    )
    delta_rows = jnp.sum(probs * d_probs, axis=-1, keepdims=True)
    d_scores = (probs * (d_probs - delta_rows)).astype(jnp.bfloat16)
    d_queries = jnp.einsum(
        "bhqk,bkhd->bqhd", d_scores, key_blocks, preferred_element_type=jnp.float32
    ) * HD ** (-0.5)
    d_keys = jnp.einsum(
        "bhqk,bqhd->bkhd", d_scores, query_blocks, preferred_element_type=jnp.float32
    ) * HD ** (-0.5)
    d_queries = d_queries.reshape(rows_all, width_c).astype(jnp.bfloat16)
    d_keys = d_keys.reshape(rows_all, width_c).astype(jnp.bfloat16)
    d_values = d_values.reshape(rows_all, width_c).astype(jnp.bfloat16)
    grad_query = jnp.einsum("td,tc->dc", normed_low, d_queries, preferred_element_type=jnp.float32)
    grad_key = jnp.einsum("td,tc->dc", normed_low, d_keys, preferred_element_type=jnp.float32)
    grad_value = jnp.einsum("td,tc->dc", normed_low, d_values, preferred_element_type=jnp.float32)
    grad_gate = jnp.einsum("td,tc->dc", normed_low, d_gate, preferred_element_type=jnp.float32)
    attn_grads = (
        lax.psum_scatter(grad_query, "dp", scatter_dimension=0, tiled=True),
        lax.psum_scatter(grad_key, "dp", scatter_dimension=0, tiled=True),
        lax.psum_scatter(grad_value, "dp", scatter_dimension=0, tiled=True),
        lax.psum_scatter(grad_gate, "dp", scatter_dimension=0, tiled=True),
        lax.psum_scatter(grad_out, "dp", scatter_dimension=1, tiled=True),
    )
    d_partial_one = jnp.einsum("tc,dc->td", d_queries, w_query, preferred_element_type=jnp.float32)
    d_partial_one = d_partial_one + jnp.einsum(
        "tc,dc->td", d_keys, w_key, preferred_element_type=jnp.float32
    )
    d_partial_one = d_partial_one + jnp.einsum(
        "tc,dc->td", d_values, w_value, preferred_element_type=jnp.float32
    )
    d_partial_one = d_partial_one + jnp.einsum(
        "tc,dc->td", d_gate, w_gate, preferred_element_type=jnp.float32
    )
    d_norm_one = head_total(d_partial_one)
    d_source = d_hidden + norm_back(d_norm_one, normed_one, recip_one)
    grad_tokens = d_source.astype(jnp.bfloat16)
    return (
        output,
        grad_tokens,
        attn_grads[0],
        attn_grads[1],
        attn_grads[2],
        attn_grads[3],
        attn_grads[4],
        glu_grads[0],
        glu_grads[1],
        glu_grads[2],
    )


def solution(mesh):
    in_specs = (
        P("dp", None),
        P("dp", None),
        P(None, "mp"),
        P(None, "mp"),
        P(None, "mp"),
        P(None, "mp"),
        P("mp", None),
        P(None, "mp"),
        P(None, "mp"),
        P("mp", None),
        P("dp", None),
    )
    out_specs = (
        P("dp", None),
        P("dp", None),
        P("dp", "mp"),
        P("dp", "mp"),
        P("dp", "mp"),
        P("dp", "mp"),
        P("mp", "dp"),
        P("dp", "mp"),
        P("dp", "mp"),
        P("mp", "dp"),
    )
    return jax.shard_map(body, mesh=mesh, in_specs=in_specs, out_specs=out_specs, check_vma=False)
```

profile of v0, /device:TPU:9, one launch (start us, length us, event | category | flops | bytes accessed | tf_op | source)
XLA Modules:
  0.0 1088.0 jit_solution(14970496762078852866)
XLA Ops:
  22.1 5.3 convolution_convert_fusion.3
  40.5 4.6 reshape.148
  57.1 6.6 copy.59
  67.3 5.4 multiply_convert_fusion.7
  77.0 86.5 %all-reduce.5.cloned.1.call-done = bf16[2048,1024]{1,0:T(8,128)(2,1)} async-done(((bf16[2048,1024]{1,0:T(8,128)(2,1)}), bf16[2048,1024]{1,0:T(8,128)(2,1)}) %all-reduce.5.cloned.1.call-update) | async-done | bytes 4194320 | tf_op jit(solution)/shard_map/psum | solution.py:11
  163.5 5.0 multiply_reduce_fusion
  177.5 5.5 multiply_convert_fusion
  183.0 6.9 fusion.38
  189.9 5.7 add_convert_fusion.1
  195.6 5.0 reshape.154
  202.1 7.2 convolution_convert_fusion
  209.3 72.0 %all-reduce.7.cloned.1.call-done = bf16[2048,1024]{1,0:T(8,128)(2,1)} async-done(((bf16[2048,1024]{1,0:T(8,128)(2,1)}), bf16[2048,1024]{1,0:T(8,128)(2,1)}) %all-reduce.7.cloned.1.call-update) | async-done | bytes 4194320 | tf_op jit(solution)/shard_map/psum | solution.py:11
  281.4 6.7 fusion.3
  289.7 5.0 fusion.5
  299.4 5.0 reshape.155
  304.5 6.6 fusion.14
  326.2 5.6 copy.69
  354.3 9.8 add_convert_fusion
  365.4 5.6 fusion.22
  390.1 7.8 fusion.47
  398.0 8.0 fusion.48
  406.3 8.1 fusion.46
  414.4 103.0 %all-reduce.9.cloned.1.call-done = (bf16[2048,1024]{1,0:T(8,128)(2,1)}, bf16[2048,1024]{1,0:T(8,128)(2,1)}) async-done(((bf16[2048,1024]{1,0:T(8,128)(2,1)}, bf16[2048,1024]{1,0:T(8,128)(2,1)}), (bf16[2048,1024]{1,0:T(8,128)(2,1)}, bf16[2048,1024]{1,0:T(8,128)(2,1)})) %all-reduce.9.cloned.1.call-update) | async-done | bytes 8388624 | tf_op jit(solution)/shard_map/psum | solution.py:11
  523.3 9.7 fusion.8
  533.0 51.1 %reduce-scatter.17.cloned.1.call-done = f32[256,128]{1,0:T(8,128)} async-done(((f32[256,1024]{1,0:T(8,128)}), f32[256,128]{1,0:T(8,128)}) %reduce-scatter.17.cloned.1.call-update) | async-done | bytes 131088 | tf_op jit(solution)/shard_map/reduce_scatter | solution.py:137
  584.1 67.0 %reduce-scatter.15.cloned.1.call-done = f32[128,256]{1,0:T(8,128)} async-done(((f32[1024,256]{1,0:T(8,128)}), f32[128,256]{1,0:T(8,128)}) %reduce-scatter.15.cloned.1.call-update) | async-done | bytes 131088 | tf_op jit(solution)/shard_map/reduce_scatter | solution.py:136
  651.1 66.9 %reduce-scatter.11.cloned.1.call-done = f32[128,256]{1,0:T(8,128)} async-done(((f32[1024,256]{1,0:T(8,128)}), f32[128,256]{1,0:T(8,128)}) %reduce-scatter.11.cloned.1.call-update) | async-done | bytes 131088 | tf_op jit(solution)/shard_map/reduce_scatter | solution.py:134
  718.0 67.1 %reduce-scatter.13.cloned.1.call-done = f32[128,256]{1,0:T(8,128)} async-done(((f32[1024,256]{1,0:T(8,128)}), f32[128,256]{1,0:T(8,128)}) %reduce-scatter.13.cloned.1.call-update) | async-done | bytes 131088 | tf_op jit(solution)/shard_map/reduce_scatter | solution.py:135
  785.1 67.1 %reduce-scatter.9.cloned.1.call-done = f32[128,256]{1,0:T(8,128)} async-done(((f32[1024,256]{1,0:T(8,128)}), f32[128,256]{1,0:T(8,128)}) %reduce-scatter.9.cloned.1.call-update) | async-done | bytes 131088 | tf_op jit(solution)/shard_map/reduce_scatter | solution.py:133
  852.3 76.5 %reduce-scatter.19.cloned.1.call-done = f32[128,704]{0,1:T(8,128)} async-done(((f32[1024,704]{0,1:T(8,128)}), f32[128,704]{0,1:T(8,128)}) %reduce-scatter.19.cloned.1.call-update) | async-done | bytes 360464 | tf_op jit(solution)/shard_map/reduce_scatter | solution.py:87
  928.8 76.2 %reduce-scatter.21.cloned.1.call-done = f32[128,704]{0,1:T(8,128)} async-done(((f32[1024,704]{0,1:T(8,128)}), f32[128,704]{0,1:T(8,128)}) %reduce-scatter.21.cloned.1.call-update) | async-done | bytes 360464 | tf_op jit(solution)/shard_map/reduce_scatter | solution.py:88
  1005.0 76.3 %reduce-scatter.23.cloned.1.call-done = f32[704,128]{1,0:T(8,128)} async-done(((f32[704,1024]{1,0:T(8,128)}), f32[704,128]{1,0:T(8,128)}) %reduce-scatter.23.cloned.1.call-update) | async-done | bytes 360464 | tf_op jit(solution)/shard_map/reduce_scatter | solution.py:89
  (174 shorter events, 128.4 us)
Async XLA Ops:
  7.2 170.3 %copy-start = (bf16[704,1024]{1,0:T(8,128)(2,1)S(1)}, bf16[704,1024]{1,0:T(8,128)(2,1)}, u32[]{:S(2)}) copy-start(bf16[704,1024]{1,0:T(8,128)(2,1)} %param.20) | copy-start | bytes 4325380
  7.2 156.3 %all-reduce.5.cloned.1.call-start = ((), (), s32[]{:S(2)}) async-start(), calls=%async_computation.8 | async-start | bytes 8388608 | tf_op jit(solution)/shard_map/psum | solution.py:11
  22.1 24.1 %copy-start.16 = (bf16[32,64,4,64]{1,3,2,0:T(8,128)(2,1)}, bf16[32,64,4,64]{1,3,2,0:T(8,128)(2,1)S(1)}, u32[]{:S(2)}) copy-start(bf16[32,64,4,64]{1,3,2,0:T(8,128)(2,1)S(1)} %copy.66) | copy-start | bytes 3145732
  49.0 6.7 copy-start.7
  49.0 6.7 copy-start.37
  67.3 6.4 copy-start.34
  77.0 204.4 %all-reduce.7.cloned.1.call-start = ((), (), s32[]{:S(2)}) async-start(), calls=%async_computation.9 | async-start | bytes 8388608 | tf_op jit(solution)/shard_map/psum | solution.py:11
  163.5 5.9 copy-start.9
  183.0 6.9 copy-start.22
  183.0 6.9 copy-start.49
  195.6 321.8 %all-reduce.9.cloned.1.call-start = ((), (), s32[]{:S(2)}) async-start(), calls=%async_computation.18 | async-start | bytes 16777216 | tf_op jit(solution)/shard_map/psum | solution.py:11
  281.4 6.7 copy-start.4
  281.4 7.1 copy-start.10
  281.4 8.3 copy-start.13
  289.7 5.1 copy-start.35
  289.7 5.1 copy-start.40
  299.3 5.2 copy-start.39
  304.5 6.6 copy-start.8
  304.5 6.6 copy-start.36
  326.2 9.0 copy-start.27
  335.2 10.0 copy-start.28
  364.2 219.9 %reduce-scatter.17.cloned.1.call-start = ((), (), s32[]{:S(2)}) async-start(), calls=%async_computation.14 | async-start | bytes 1179648 | tf_op jit(solution)/shard_map/reduce_scatter | solution.py:137
  371.1 280.1 %reduce-scatter.15.cloned.1.call-start = ((), (), s32[]{:S(2)}) async-start(), calls=%async_computation.13 | async-start | bytes 1179648 | tf_op jit(solution)/shard_map/reduce_scatter | solution.py:136
  375.8 342.3 %reduce-scatter.11.cloned.1.call-start = ((), (), s32[]{:S(2)}) async-start(), calls=%async_computation.11 | async-start | bytes 1179648 | tf_op jit(solution)/shard_map/reduce_scatter | solution.py:134
  380.8 404.4 %reduce-scatter.13.cloned.1.call-start = ((), (), s32[]{:S(2)}) async-start(), calls=%async_computation.12 | async-start | bytes 1179648 | tf_op jit(solution)/shard_map/reduce_scatter | solution.py:135
  385.5 466.8 %reduce-scatter.9.cloned.1.call-start = ((), (), s32[]{:S(2)}) async-start(), calls=%async_computation.10 | async-start | bytes 1179648 | tf_op jit(solution)/shard_map/reduce_scatter | solution.py:133
  390.1 538.7 %reduce-scatter.19.cloned.1.call-start = ((), (), s32[]{:S(2)}) async-start(), calls=%async_computation.15 | async-start | bytes 3244032 | tf_op jit(solution)/shard_map/reduce_scatter | solution.py:87
  397.9 607.1 %reduce-scatter.21.cloned.1.call-start = ((), (), s32[]{:S(2)}) async-start(), calls=%async_computation.16 | async-start | bytes 3244032 | tf_op jit(solution)/shard_map/reduce_scatter | solution.py:88
  406.1 111.3 %copy-start.46 = (f32[2048]{0:T(1024)S(1)}, f32[2048]{0:T(1024)}, u32[]{:S(2)}) copy-start(f32[2048]{0:T(1024)} %copy-done.45) | copy-start | bytes 24580
  406.1 675.2 %reduce-scatter.23.cloned.1.call-start = ((), (), s32[]{:S(2)}) async-start(), calls=%async_computation.17 | async-start | bytes 3244032 | tf_op jit(solution)/shard_map/reduce_scatter | solution.py:89
  517.4 5.9 copy-start.11
  523.3 558.0 %copy-start.1 = (bf16[704,1024]{1,0:T(8,128)(2,1)S(1)}, bf16[704,1024]{1,0:T(8,128)(2,1)}, u32[]{:S(2)}) copy-start(bf16[704,1024]{1,0:T(8,128)(2,1)} %param.20) | copy-start | bytes 4325380
  (29 other events, 91.4 us)
Sparse Core Ops, SparseCore 0:
  77.1 86.3 all-reduce.4
  195.7 85.6 all-reduce.6
  364.3 153.0 all-reduce.8
  521.2 62.8 reduce-scatter.16
  587.9 63.1 reduce-scatter.14
  655.0 63.0 reduce-scatter.10
  722.0 63.0 reduce-scatter.12
  789.1 63.1 reduce-scatter.8
  856.4 72.3 reduce-scatter.18
  932.8 72.2 reduce-scatter.20
  1009.2 72.0 reduce-scatter.22
where the time goes:
time: 1100 us; the launch traced here: 1090 us
  waiting for transfers between devices  810 us (74%)
  matrix products  139 us (13%)
  local copies, waits for them, and re-layouts  71.3 us (6%)
  other arithmetic  51.9 us (5%)
  between operations  14.7 us (1%)
    psum x3, waiting for transfers between devices, head_total(): lax.psum(partial_value.astype(jnp.bfloat16), 'mp').astype(jnp.float32)  261 us
    reduce_scatter x1, waiting for transfers between devices, body(): lax.psum_scatter(grad_left, 'dp', scatter_dimension=0, tiled=True)  76.5 us
    reduce_scatter x1, waiting for transfers between devices, body(): lax.psum_scatter(grad_down, 'dp', scatter_dimension=1, tiled=True)  76.3 us
    reduce_scatter x1, waiting for transfers between devices, body(): lax.psum_scatter(grad_right, 'dp', scatter_dimension=0, tiled=True)  76.2 us
    reduce_scatter x1, waiting for transfers between devices, body(): lax.psum_scatter(grad_query, 'dp', scatter_dimension=0, tiled=True)  67.1 us
    reduce_scatter x1, waiting for transfers between devices, body(): lax.psum_scatter(grad_value, 'dp', scatter_dimension=0, tiled=True)  67.1 us
    reduce_scatter x1, waiting for transfers between devices, body(): lax.psum_scatter(grad_gate, 'dp', scatter_dimension=0, tiled=True)  67 us
    reduce_scatter x1, waiting for transfers between devices, body(): lax.psum_scatter(grad_key, 'dp', scatter_dimension=0, tiled=True)  66.9 us
  transfers between devices with their start and end apart: 11, of which 11 were waited for; matrix products, arithmetic and copies ran while one was open for 7% of the time, Pallas kernels for 0%

commit v1 on v0

--- a/solution.py
+++ b/solution.py
@@ -9,6 +9,17 @@
 
 def head_total(partial_value):
     return lax.psum(partial_value.astype(jnp.bfloat16), "mp").astype(jnp.float32)
+
+
+def scatter_sum(grads):
+    joined = jnp.concatenate([g.astype(jnp.bfloat16) for g in grads], axis=1)
+    summed = lax.psum_scatter(joined, "dp", scatter_dimension=0, tiled=True).astype(jnp.float32)
+    cuts = []
+    at = 0
+    for g in grads:
+        cuts.append(summed[:, at : at + g.shape[1]])
+        at += g.shape[1]
+    return cuts
 
 
 def rms_factor(values):
@@ -75,7 +86,7 @@
     mixed = (left * right).astype(jnp.bfloat16)
     glu_sum = head_total(jnp.dot(mixed, w_down, preferred_element_type=jnp.float32))
     output = (hidden + glu_sum).astype(jnp.bfloat16)
-    grad_down = jnp.einsum("tf,tc->fc", mixed, cotangent, preferred_element_type=jnp.float32)
+    grad_down = jnp.einsum("tc,tf->cf", cotangent, mixed, preferred_element_type=jnp.float32)
     d_mixed = jnp.einsum("tc,fc->tf", cotangent, w_down, preferred_element_type=jnp.float32)
     d_left = (d_mixed * right).astype(jnp.bfloat16)
     d_right = (d_mixed * left).astype(jnp.bfloat16)
@@ -83,11 +94,7 @@
     grad_right = jnp.einsum(
         "td,tf->df", normed_two_low, d_right, preferred_element_type=jnp.float32
     )
-    glu_grads = (
-        lax.psum_scatter(grad_left, "dp", scatter_dimension=0, tiled=True),
-        lax.psum_scatter(grad_right, "dp", scatter_dimension=0, tiled=True),
-        lax.psum_scatter(grad_down, "dp", scatter_dimension=1, tiled=True),
-    )
+    glu_grads = scatter_sum((grad_left, grad_right, grad_down))
     d_partial_two = jnp.einsum("tf,df->td", d_left, w_left, preferred_element_type=jnp.float32)
     d_partial_two = d_partial_two + jnp.einsum(
         "tf,df->td", d_right, w_right, preferred_element_type=jnp.float32
@@ -95,7 +102,7 @@
     d_norm_two = head_total(d_partial_two)
     d_hidden = cotangent.astype(jnp.float32) + norm_back(d_norm_two, normed_two, recip_two)
     d_out_low = d_hidden.astype(jnp.bfloat16)
-    grad_out = jnp.einsum("tc,td->cd", gated, d_out_low, preferred_element_type=jnp.float32)
+    grad_out = jnp.einsum("td,tc->dc", d_out_low, gated, preferred_element_type=jnp.float32)
     d_gated = jnp.einsum("td,cd->tc", d_out_low, w_out, preferred_element_type=jnp.float32)
     d_gated = d_gated.reshape(rows_all, heads_here, HD)
     d_head = d_gated * sigma
@@ -129,13 +136,7 @@
     grad_key = jnp.einsum("td,tc->dc", normed_low, d_keys, preferred_element_type=jnp.float32)
     grad_value = jnp.einsum("td,tc->dc", normed_low, d_values, preferred_element_type=jnp.float32)
     grad_gate = jnp.einsum("td,tc->dc", normed_low, d_gate, preferred_element_type=jnp.float32)
-    attn_grads = (
-        lax.psum_scatter(grad_query, "dp", scatter_dimension=0, tiled=True),
-        lax.psum_scatter(grad_key, "dp", scatter_dimension=0, tiled=True),
-        lax.psum_scatter(grad_value, "dp", scatter_dimension=0, tiled=True),
-        lax.psum_scatter(grad_gate, "dp", scatter_dimension=0, tiled=True),
-        lax.psum_scatter(grad_out, "dp", scatter_dimension=1, tiled=True),
-    )
+    attn_grads = scatter_sum((grad_query, grad_key, grad_value, grad_gate, grad_out))
     d_partial_one = jnp.einsum("tc,dc->td", d_queries, w_query, preferred_element_type=jnp.float32)
     d_partial_one = d_partial_one + jnp.einsum(
         "tc,dc->td", d_keys, w_key, preferred_element_type=jnp.float32
@@ -156,10 +157,10 @@
         attn_grads[1],
         attn_grads[2],
         attn_grads[3],
-        attn_grads[4],
+        attn_grads[4].T,
         glu_grads[0],
         glu_grads[1],
-        glu_grads[2],
+        glu_grads[2].T,
     )
 
 

time: 1100 us -> 705 us (0.64)
  waiting for transfers between devices: 810 us -> 421 us
  matrix products: 139 us -> 116 us
  local copies, waits for them, and re-layouts: 71.3 us -> 89 us
    reduce_scatter x8 -> x0, waiting for transfers between devices: 548 us -> none  [the longest x1 76.5 us: body(): lax.psum_scatter(grad_left, 'dp', scatter_dimension=0, tiled=True)]
    unnamed x11 -> x7, waiting for transfers between devices: 0.18 us -> 149 us
    unnamed x101 -> x123, local copies, waits for them, and re-layouts: 12.3 us -> 27.9 us
  transfers between devices with their start and end apart: 11 -> 5, of which waited for: 11 -> 5; matrix products, arithmetic and copies ran while one was open for 7% -> 10% of each run, Pallas kernels for 0% -> 0%
where the time goes in v1:
time: 705 us; the launch traced here: 695 us
  waiting for transfers between devices  421 us (60%)
  matrix products  116 us (16%)
  local copies, waits for them, and re-layouts  89 us (13%)
  other arithmetic  54.2 us (8%)
  between operations  14.7 us (2%)
    psum x3, waiting for transfers between devices, head_total(): lax.psum(partial_value.astype(jnp.bfloat16), 'mp').astype(jnp.float32)  272 us
    unnamed x7, waiting for transfers between devices  149 us
    unnamed x123, local copies, waits for them, and re-layouts  27.9 us
  transfers between devices with their start and end apart: 5, of which 5 were waited for; matrix products, arithmetic and copies ran while one was open for 10% of the time, Pallas kernels for 0%

profile of v1, /device:TPU:9, one launch (start us, length us, event | category | flops | bytes accessed | tf_op | source)
XLA Modules:
  0.0 695.0 jit_solution(10704735771133625387)
XLA Ops:
  22.1 5.3 convolution_convert_fusion.3
  27.4 4.4 reshape.149
  36.0 4.5 convolution_convert_fusion.4
  40.5 4.6 reshape.148
  57.0 6.6 copy.67
  67.3 5.4 multiply_convert_fusion.7
  77.0 86.4 %all-reduce.5.cloned.1.call-done = bf16[2048,1024]{1,0:T(8,128)(2,1)} async-done(((bf16[2048,1024]{1,0:T(8,128)(2,1)}), bf16[2048,1024]{1,0:T(8,128)(2,1)}) %all-reduce.5.cloned.1.call-update) | async-done | bytes 4194320 | tf_op jit(solution)/shard_map/psum | solution.py:11
  163.4 5.0 multiply_reduce_fusion
  177.4 5.5 multiply_convert_fusion
  182.9 6.0 fusion.51
  188.9 5.7 add_convert_fusion.1
  194.7 5.0 reshape.154
  201.2 7.2 %convolution_convert_fusion = bf16[2048,1024]{1,0:T(8,128)(2,1)} fusion(bf16[2048,704]{0,1:T(8,128)(2,1)} %get-tuple-element.45, bf16[704,1024]{1,0:T(8,128)(2,1)S(1)} %copy-done), kind=kOutput, calls=%fused_computation.39 | convolution fusion | flops 2954887168 | bytes 8519680 | tf_op jit(solution)/shard_map/dot_general | solution.py:87
  208.4 72.1 %all-reduce.7.cloned.1.call-done = bf16[2048,1024]{1,0:T(8,128)(2,1)} async-done(((bf16[2048,1024]{1,0:T(8,128)(2,1)}), bf16[2048,1024]{1,0:T(8,128)(2,1)}) %all-reduce.7.cloned.1.call-update) | async-done | bytes 4194320 | tf_op jit(solution)/shard_map/psum | solution.py:11
  280.4 6.6 fusion.3
  288.8 5.0 fusion.5
  298.5 5.0 reshape.155
  303.6 6.6 fusion.14
  324.5 5.9 copy.77
  330.4 4.2 convert_element_type.166
  344.3 4.7 fusion.53
  349.0 4.6 fusion.52
  353.6 9.9 %add_convert_fusion = bf16[2048,1024]{1,0:T(8,128)(2,1)} fusion(f32[2048,1024]{1,0:T(8,128)S(1)} %fusion.54, f32[2048,1024]{1,0:T(8,128)} %fusion.52, f32[2048,1024]{1,0:T(8,128)} %fusion.53, bf16[2048,256]{0,1:T(8,128)(2,1)S(1)} %copy-done.36, bf16[1024,256]{1,0:T(8,128)(2,1)S(1)} %copy-done.38), kind=kOutput, calls=%fused_computation.17 | convolution fusion | flops 1082130432 | bytes 30932992 | tf_op jit(solution)/shard_map/tc,dc->td/dot_general | solution.py:147
  363.6 4.4 fusion.45
  376.4 4.5 copy.95
  381.1 6.3 convolution_convert_fusion.5
  396.3 6.6 copy.97
  402.9 113.8 %all-reduce.9.cloned.1.call-done = (bf16[2048,1024]{1,0:T(8,128)(2,1)}, bf16[2048,1024]{1,0:T(8,128)(2,1)}) async-done(((bf16[2048,1024]{1,0:T(8,128)(2,1)}, bf16[2048,1024]{1,0:T(8,128)(2,1)}), (bf16[2048,1024]{1,0:T(8,128)(2,1)}, bf16[2048,1024]{1,0:T(8,128)(2,1)})) %all-reduce.9.cloned.1.call-update) | async-done | bytes 8388624 | tf_op jit(solution)/shard_map/psum | solution.py:11
  516.7 4.5 fusion.9
  522.6 9.6 %fusion.8 = (bf16[2048,1024]{1,0:T(8,128)(2,1)}, bf16[2048,1024]{1,0:T(8,128)(2,1)}) fusion(f32[2048,1024]{1,0:T(8,128)} %copy-done.6, bf16[2048,1024]{1,0:T(8,128)(2,1)} %get-tuple-element.41, bf16[2048,1024]{1,0:T(8,128)(2,1)S(1)} %copy-done.5, f32[2048]{0:T(1024)S(1)} %broadcast_multiply_fusion.1, f32[2048]{0:T(1024)S(1)} %copy-done.51, ...), kind=kLoop, calls=%fused_computation.14 | loop fusion | flops 27262976 | bytes 33570816 | tf_op jit(solution)/shard_map/convert_element_type | solution.py:152
  532.2 57.2 %reduce-scatter.7.cloned.1.call-done = bf16[128,1280]{1,0:T(8,128)(2,1)} async-done(((bf16[1024,1280]{1,0:T(8,128)(2,1)}), bf16[128,1280]{1,0:T(8,128)(2,1)}) %reduce-scatter.7.cloned.1.call-update) | async-done | bytes 327696
  594.5 91.4 %reduce-scatter.9.cloned.1.call-done = bf16[128,2112]{1,0:T(8,128)(2,1)} async-done(((bf16[1024,2112]{1,0:T(8,128)(2,1)}), bf16[128,2112]{1,0:T(8,128)(2,1)}) %reduce-scatter.9.cloned.1.call-update) | async-done | bytes 540688
  (185 shorter events, 105.9 us)
Async XLA Ops:
  7.2 170.2 %copy-start = (bf16[704,1024]{1,0:T(8,128)(2,1)S(1)}, bf16[704,1024]{1,0:T(8,128)(2,1)}, u32[]{:S(2)}) copy-start(bf16[704,1024]{1,0:T(8,128)(2,1)} %param.20) | copy-start | bytes 4325380
  7.2 156.2 %all-reduce.5.cloned.1.call-start = ((), (), s32[]{:S(2)}) async-start(), calls=%async_computation.2 | async-start | bytes 8388608 | tf_op jit(solution)/shard_map/psum | solution.py:11
  22.1 24.0 %copy-start.17 = (bf16[32,64,4,64]{1,3,2,0:T(8,128)(2,1)}, bf16[32,64,4,64]{1,3,2,0:T(8,128)(2,1)S(1)}, u32[]{:S(2)}) copy-start(bf16[32,64,4,64]{1,3,2,0:T(8,128)(2,1)S(1)} %copy.74) | copy-start | bytes 3145732
  48.9 6.7 copy-start.7
  49.0 6.7 copy-start.42
  67.3 6.3 copy-start.39
  77.0 203.5 %all-reduce.7.cloned.1.call-start = ((), (), s32[]{:S(2)}) async-start(), calls=%async_computation.3 | async-start | bytes 8388608 | tf_op jit(solution)/shard_map/psum | solution.py:11
  163.4 5.0 copy-start.3
  163.4 5.9 copy-start.9
  182.9 6.0 copy-start.25
  182.9 6.0 copy-start.27
  182.9 6.0 copy-start.54
  194.7 322.0 %all-reduce.9.cloned.1.call-start = ((), (), s32[]{:S(2)}) async-start(), calls=%async_computation.6 | async-start | bytes 16777216 | tf_op jit(solution)/shard_map/psum | solution.py:11
  280.4 6.7 copy-start.4
  280.4 7.1 %copy-start.10 = (bf16[2048,1024]{1,0:T(8,128)(2,1)S(1)}, bf16[2048,1024]{1,0:T(8,128)(2,1)}, u32[]{:S(2)}) copy-start(bf16[2048,1024]{1,0:T(8,128)(2,1)} %all-reduce.5.cloned.1.call-done) | copy-start | bytes 12582916
  280.4 8.3 %copy-start.13 = (bf16[2048,1024]{1,0:T(8,128)(2,1)S(1)}, bf16[2048,1024]{1,0:T(8,128)(2,1)}, u32[]{:S(2)}) copy-start(bf16[2048,1024]{1,0:T(8,128)(2,1)} %param.21) | copy-start | bytes 12582916
  288.8 5.1 copy-start.15
  288.8 5.1 copy-start.29
  288.8 5.1 copy-start.40
  288.8 5.1 copy-start.45
  298.4 5.2 copy-start.44
  303.6 6.6 copy-start.8
  303.6 6.6 copy-start.41
  324.5 10.1 %copy-start.32 = (bf16[32,64,4,64]{3,1,2,0:T(8,128)(2,1)S(1)}, bf16[32,64,4,64]{3,1,2,0:T(8,128)(2,1)}, u32[]{:S(2)}) copy-start(bf16[32,64,4,64]{3,1,2,0:T(8,128)(2,1)} %fusion.34) | copy-start | bytes 3145732
  363.5 225.8 %reduce-scatter.7.cloned.1.call-start = ((), (), s32[]{:S(2)}) async-start(), calls=%async_computation.4 | async-start | bytes 2949120
  368.0 6.3 slice-start
  380.9 305.0 %reduce-scatter.9.cloned.1.call-start = ((), (), s32[]{:S(2)}) async-start(), calls=%async_computation.5 | async-start | bytes 5013504
  381.1 6.4 copy-start.26
  381.1 6.4 copy-start.35
  402.8 113.9 %copy-start.51 = (f32[2048]{0:T(1024)S(1)}, f32[2048]{0:T(1024)}, u32[]{:S(2)}) copy-start(f32[2048]{0:T(1024)} %copy-done.50) | copy-start | bytes 24580
  516.7 5.9 copy-start.11
  589.4 98.9 %copy-start.1 = (bf16[704,1024]{1,0:T(8,128)(2,1)S(1)}, bf16[704,1024]{1,0:T(8,128)(2,1)}, u32[]{:S(2)}) copy-start(bf16[704,1024]{1,0:T(8,128)(2,1)} %param.20) | copy-start | bytes 4325380
  (30 other events, 88.8 us)
Sparse Core Ops, SparseCore 0:
  77.1 86.3 all-reduce.4
  194.8 85.6 all-reduce.6
  363.7 153.0 all-reduce.8
  520.1 69.2 reduce-scatter.6
  592.8 92.9 reduce-scatter.8

commit v2 on v1

v2 whole, which is shorter than its diff:
```python
import functools

import jax
import jax.numpy as jnp
from jax import lax
from jax.experimental import pallas as pl
from jax.experimental.pallas import tpu as pltpu
from jax.sharding import PartitionSpec as P

HD = 64
BLOCK = 64
CHUNK = 256
TILE = 128
RING = 4
EPS = 1e-06
F32 = jnp.float32
BF16 = jnp.bfloat16
MESH = pl.DeviceIdType.MESH


def dot_nn(a, b):
    return lax.dot_general(a, b, (((1,), (0,)), ((), ())), preferred_element_type=F32)


def dot_nt(a, b):
    return lax.dot_general(a, b, (((1,), (1,)), ((), ())), preferred_element_type=F32)


def dot_tn(a, b):
    return lax.dot_general(a, b, (((0,), (0,)), ((), ())), preferred_element_type=F32)


def rms_factor(v):
    return lax.rsqrt(jnp.mean(v * v, axis=-1, keepdims=True) + EPS)


def norm_back(grad, normed, factor):
    return factor * (grad - normed * jnp.mean(grad * normed, axis=-1, keepdims=True))


def mult(v, n):
    return pl.multiple_of(v, n)


class Refs:
    pass


def kernel(names, ndp, *refs):
    r = Refs()
    for name, ref in zip(names, refs):
        setattr(r, name, ref)
    tokens, width = r.n1.shape
    chunks = tokens // CHUNK
    half, quarter = CHUNK // 2, CHUNK // 4
    wc = r.wo.shape[0]
    fp = r.wl.shape[1]
    ff = r.wl_h.shape[1]
    block_rows = width // ndp
    pairs = ndp // 2
    groups = width // 256
    per_group = pairs // groups
    half_chunks = chunks // 2
    wide = 5 * wc // 2

    dp = lax.axis_index("dp")
    mp = lax.axis_index("mp")
    core = mp % 2
    side = mp // 2
    partner = (dp, mp + 1 - 2 * core)
    across = (dp, mp + 2 - 4 * side)
    parity = dp % 2
    line = dp // 2
    beside = (dp + 1 - 2 * parity, mp)

    def remote(src, dst, send, recv, device):
        return pltpu.make_async_remote_copy(
            src_ref=src,
            dst_ref=dst,
            send_sem=send,
            recv_sem=recv,
            device_id=device,
            device_id_type=MESH,
        )

    barrier = pltpu.get_barrier_semaphore()
    for device in (partner, across, beside):
        pl.semaphore_signal(barrier, inc=1, device_id=device, device_id_type=MESH)

    def greet(j, carry):
        @pl.when(j != line)
        def _():
            pl.semaphore_signal(
                barrier, inc=1, device_id=(2 * j + parity, mp), device_id_type=MESH
            )

        return carry

    lax.fori_loop(0, pairs, greet, 0)

    def load_tokens(c):
        rows = pl.ds(mult(c * CHUNK, CHUNK), CHUNK)
        return pltpu.make_async_copy(r.tok_h.at[rows], r.n1.at[rows], r.sem_tok.at[c])

    def load_stage(i):
        src = r.wl_h if i < 2 else r.wr_h
        return pltpu.make_async_copy(
            src.at[pl.ds((i % 2) * (width // 2), width // 2)], r.stage, r.sem_w.at[7]
        )

    load_tokens(0).start()
    w_loads = [
        pltpu.make_async_copy(h, r.w.at[:, pl.ds(i * wc, wc)], r.sem_w.at[i])
        for i, h in enumerate((r.wq_h, r.wk_h, r.wv_h, r.wg_h))
    ]
    for copy in w_loads:
        copy.start()
    wo_load = pltpu.make_async_copy(r.wo_h, r.wo, r.sem_w.at[4])
    wo_load.start()
    for c in range(1, chunks):
        load_tokens(c).start()
    load_stage(0).start()
    wd_load = pltpu.make_async_copy(r.wd_h, r.wd.at[pl.ds(0, ff)], r.sem_w.at[5])
    wd_load.start()
    cot_load = pltpu.make_async_copy(r.cot_h, r.cot, r.sem_w.at[6])
    cot_load.start()

    pl.semaphore_wait(barrier, 3 + pairs - 1)

    def base(c):
        return mult(c * CHUNK, CHUNK)

    def own_rows(c):
        return pl.ds(mult(c * CHUNK + core * half + side * quarter, quarter), quarter)

    def other_rows(c):
        return pl.ds(mult(c * CHUNK + core * half + (1 - side) * quarter, quarter), quarter)

    def partner_own_rows(c):
        return pl.ds(mult(c * CHUNK + (1 - core) * half + side * quarter, quarter), quarter)

    def partner_other_rows(c):
        return pl.ds(mult(c * CHUNK + (1 - core) * half + (1 - side) * quarter, quarter), quarter)

    def kept(c):
        return pl.ds(mult(c * quarter, quarter), quarter)

    def part_of(s):
        return r.part_g if s == 1 else r.part

    def pair_of(s):
        return r.pair_g if s == 1 else r.pair

    def sent_of(s):
        return r.sent_g if s == 1 else r.sent

    def got_of(s):
        return r.got_g if s == 1 else r.got

    def full_of(s):
        return (r.n2, r.out_h, r.do, r.gt_h)[s]

    def at(s, c):
        return s * chunks + c

    def pair_copy(s, c):
        slot = c % RING
        return remote(
            part_of(s).at[c % 2, pl.ds(mult((1 - core) * half, half), half)],
            pair_of(s).at[slot],
            r.sem_as.at[at(s, c)],
            r.sem_ar.at[at(s, c)],
            partner,
        )

    def across_copy(s, c):
        return remote(
            sent_of(s).at[kept(c)],
            got_of(s).at[kept(c)],
            r.sem_bs.at[at(s, c)],
            r.sem_br.at[at(s, c)],
            across,
        )

    def result_src(s, c):
        if s in (0, 2):
            return full_of(s).at[own_rows(c)]
        return sent_of(s).at[kept(c)]

    def result_across(s, c):
        return remote(
            result_src(s, c),
            full_of(s).at[own_rows(c)],
            r.sem_cs.at[at(s, c)],
            r.sem_cr.at[at(s, c)],
            across,
        )

    def result_partner(s, c):
        return remote(
            result_src(s, c),
            full_of(s).at[own_rows(c)],
            r.sem_ps.at[at(s, c)],
            r.sem_pr.at[at(s, c)],
            partner,
        )

    def result_own(s, c):
        return pltpu.make_async_copy(
            sent_of(s).at[kept(c)], full_of(s).at[own_rows(c)], r.sem_o.at[at(s // 2, c)]
        )

    def forward(s, c):
        return remote(
            full_of(s).at[other_rows(c)],
            full_of(s).at[other_rows(c)],
            r.sem_ds.at[at(s, c)],
            r.sem_dr.at[at(s, c)],
            partner,
        )

    def step_b(s, c, send=True):
        copy = pair_copy(s, c)
        copy.wait_recv()
        copy.wait_send()
        part, pair = part_of(s), pair_of(s)
        slot, ring = c % 2, c % RING

        def piece(i, carry):
            rows = mult(i * 32, 32)
            away = pl.ds(mult(core * half + (1 - side) * quarter + rows, 32), 32)
            away_pair = pl.ds(mult((1 - side) * quarter + rows, 32), 32)
            total = part[slot, away, :].astype(F32) + pair[ring, away_pair, :].astype(F32)
            sent_of(s)[pl.ds(mult(c * quarter + rows, 32), 32), :] = total.astype(BF16)
            mine = pl.ds(mult(core * half + side * quarter + rows, 32), 32)
            mine_pair = pl.ds(mult(side * quarter + rows, 32), 32)
            total = part[slot, mine, :].astype(F32) + pair[ring, mine_pair, :].astype(F32)
            if s == 1:
                r.own_g[pl.ds(mult(c * quarter + rows, 32), 32), :] = total.astype(BF16)
            else:
                r.own[slot, pl.ds(rows, 32), :] = total
            return carry

        lax.fori_loop(0, quarter // 32, piece, 0)
        if send:
            across_copy(s, c).start()

    def step_c(s, c):
        copy = across_copy(s, c)
        copy.wait_recv()
        copy.wait_send()
        slot = c % 2

        def piece(i, carry):
            rows = mult(i * 32, 32)
            mine = pl.ds(mult(c * quarter + rows, 32), 32)
            full = pl.ds(mult(c * CHUNK + core * half + side * quarter + rows, 32), 32)
            arrived = got_of(s)[mine, :].astype(F32)
            if s == 1:
                total = r.own_g[mine, :].astype(F32) + arrived
            else:
                total = r.own[slot, pl.ds(rows, 32), :] + arrived
            if s == 0:
                hidden = r.tok_own[mine, :].astype(F32) + total
                r.hidden[mine, :] = hidden
                r.n2[full, :] = (hidden * rms_factor(hidden)).astype(BF16)
            elif s == 1:
                r.sent_g[mine, :] = (r.hidden[mine, :] + total).astype(BF16)
            elif s == 2:
                hidden = r.hidden[mine, :]
                factor = rms_factor(hidden)
                d_hidden = r.cot[full, :].astype(F32) + norm_back(total, hidden * factor, factor)
                r.d_hidden[mine, :] = d_hidden
                r.do[full, :] = d_hidden.astype(BF16)
            else:
                source = r.tok_own[mine, :].astype(F32)
                factor = rms_factor(source)
                d_source = r.d_hidden[mine, :] + norm_back(total, source * factor, factor)
                r.sent[mine, :] = d_source.astype(BF16)
            return carry

        lax.fori_loop(0, quarter // 32, piece, 0)
        result_across(s, c).start()
        result_partner(s, c).start()
        if s in (1, 3):
            result_own(s, c).start()

    def step_d(s, c):
        result_across(s, c).wait_recv()
        forward(s, c).start()

    def step_e(s, c):
        remote(
            result_src(s, c),
            full_of(s).at[partner_own_rows(c)],
            r.sem_ps.at[at(s, c)],
            r.sem_pr.at[at(s, c)],
            partner,
        ).wait_recv()
        remote(
            full_of(s).at[other_rows(c)],
            full_of(s).at[partner_other_rows(c)],
            r.sem_ds.at[at(s, c)],
            r.sem_dr.at[at(s, c)],
            partner,
        ).wait_recv()
        result_across(s, c).wait_send()
        result_partner(s, c).wait_send()
        forward(s, c).wait_send()
        if s in (1, 3):
            result_own(s, c).wait()

    def tick(s, c):
        @pl.when(c >= 1)
        def _():
            step_b(s, c - 1)

        @pl.when(c >= 2)
        def _():
            step_c(s, c - 2)

        @pl.when(c >= 3)
        def _():
            step_d(s, c - 3)

    def late_tick(s, n):
        if n == 0:
            step_b(s, chunks - 1)
        if n <= 1:
            step_c(s, chunks - 2 + n)
        step_d(s, chunks - 3 + n)

    lane = lax.broadcasted_iota(jnp.int32, (TILE, TILE), 1)
    row = lax.broadcasted_iota(jnp.int32, (TILE, TILE), 0)
    first = lane < HD

    def stacked(v):
        zero = jnp.zeros_like(v)
        return jnp.concatenate([jnp.where(first, v, zero), jnp.where(first, zero, v)], axis=0)

    def unstacked(v):
        return jnp.where(first, v[:TILE], v[TILE:])

    def head_mean(v):
        zero = jnp.zeros_like(v)
        low = jnp.sum(jnp.where(first, v, zero), axis=-1, keepdims=True)
        high = jnp.sum(jnp.where(first, zero, v), axis=-1, keepdims=True)
        return jnp.where(first, low, high) * (1.0 / HD)

    def probs_of(tile, rows, lanes):
        ids = r.seg[pl.ds(tile, 1), :].astype(F32)
        across_ids = jnp.broadcast_to(ids, (TILE, TILE))
        allowed = (
            (across_ids == across_ids.T) & (lane <= row) & (lane // BLOCK == row // BLOCK)
        )
        stack = stacked(r.qkv[rows, pl.ds(lanes, TILE)])
        keys = r.qkv[rows, pl.ds(wc + lanes, TILE)]
        scores = dot_nt(stack, keys) * HD ** (-0.5)
        allowed2 = jnp.concatenate([allowed, allowed], axis=0)
        masked = jnp.where(allowed2, scores, F32(-1e30))
        top = jnp.max(masked, axis=-1, keepdims=True)
        expd = jnp.exp(masked - top)
        probs = expd * (1.0 / jnp.sum(expd, axis=-1, keepdims=True))
        return probs, stack, keys

    head_pairs = wc // TILE
    tiles = CHUNK // TILE

    def tile_of(c, i):
        tile = c * tiles + i // head_pairs
        lanes = mult((i % head_pairs) * TILE, TILE)
        rows = pl.ds(mult(tile * TILE, TILE), TILE)
        return tile, rows, lanes

    for copy in w_loads:
        copy.wait()
    wo_load.wait()

    def phase_one(c, carry):
        rows_all = pl.ds(base(c), CHUNK)
        load_tokens(c).wait()
        r.tok_own[kept(c), :] = r.n1[own_rows(c), :]

        def norm_piece(i, carry2):
            rows = pl.ds(mult(c * CHUNK + i * 32, 32), 32)
            x = r.n1[rows, :].astype(F32)
            r.n1[rows, :] = (x * rms_factor(x)).astype(BF16)
            return carry2

        lax.fori_loop(0, CHUNK // 32, norm_piece, 0)

        def project(t, carry2):
            cols = pl.ds(mult(t * wc, wc), wc)
            r.qkv[rows_all, cols] = dot_nn(r.n1[rows_all, :], r.w[:, cols]).astype(BF16)
            return carry2

        lax.fori_loop(0, 3, project, 0)
        r.gate_now[...] = dot_nn(r.n1[rows_all, :], r.w[:, pl.ds(3 * wc, wc)])
        r.gate[rows_all, :] = r.gate_now[...].astype(BF16)

        def attend(i, carry2):
            tile, rows, lanes = tile_of(c, i)
            probs, _, _ = probs_of(tile, rows, lanes)
            values = r.qkv[rows, pl.ds(2 * wc + lanes, TILE)]
            attended = unstacked(dot_nn(probs.astype(BF16), values))
            r.attended[rows, pl.ds(lanes, TILE)] = attended.astype(BF16)
            factor = lax.rsqrt(head_mean(attended * attended) + EPS)
            near = pl.ds(mult((i // head_pairs) * TILE, TILE), TILE)
            sigma = jax.nn.sigmoid(r.gate_now[near, pl.ds(lanes, TILE)])
            r.gated[rows, pl.ds(lanes, TILE)] = (attended * factor * sigma).astype(BF16)
            return carry2

        lax.fori_loop(0, tiles * head_pairs, attend, 0)

        def out_piece(t, carry2):
            cols = pl.ds(mult(t * 256, 256), 256)
            r.part[c % 2, :, cols] = dot_nn(r.gated[rows_all, :], r.wo[:, cols]).astype(BF16)
            return carry2

        lax.fori_loop(0, width // 256, out_piece, 0)
        pair_copy(0, c).start()

        for i in range(4):

            @pl.when(c == i)
            def _():
                load_stage(i).wait()
                dst = r.wl if i < 2 else r.wr
                start = (i % 2) * (width // 2)
                for k in range(4):
                    rows = pl.ds(start + k * (width // 8), width // 8)
                    dst[rows, pl.ds(fp - 128, 128)] = jnp.zeros((width // 8, 128), BF16)
                    dst[rows, pl.ds(0, ff)] = r.stage[pl.ds(k * (width // 8), width // 8), :]
                if i < 3:
                    load_stage(i + 1).start()

        tick(0, c)
        return carry

    lax.fori_loop(0, chunks, phase_one, 0)

    wd_load.wait()
    r.wd[pl.ds(ff, fp - ff), :] = jnp.zeros((fp - ff, width), BF16)
    cot_load.wait()

    def phase_two(c, carry):
        for n in range(3):

            @pl.when(c == n)
            def _():
                late_tick(0, n)

        step_e(0, c)
        rows_all = pl.ds(base(c), CHUNK)
        rows_half = pl.ds(mult((c % half_chunks) * CHUNK, CHUNK), CHUNK)

        def hidden_units(t, carry2):
            cols = pl.ds(mult(t * 256, 256), 256)
            left = dot_nn(r.n2[rows_all, :], r.wl[:, cols])
            right = dot_nn(r.n2[rows_all, :], r.wr[:, cols])
            r.mixed[rows_all, cols] = (left * right).astype(BF16)
            d_mixed = dot_nt(r.cot[rows_all, :], r.wd[cols, :])
            r.d_left[rows_all, cols] = (d_mixed * right).astype(BF16)
            r.d_right[c // half_chunks, rows_half, cols] = (d_mixed * left).astype(BF16)
            return carry2

        lax.fori_loop(0, fp // 256, hidden_units, 0)

        def parts(t, carry2):
            cols = pl.ds(mult(t * 256, 256), 256)
            back = dot_nt(r.d_left[rows_all, :], r.wl[cols, :])
            back = back + dot_nt(r.d_right[c // half_chunks, rows_half, :], r.wr[cols, :])
            r.part[c % 2, :, cols] = back.astype(BF16)
            r.part_g[c % 2, :, cols] = dot_nn(r.mixed[rows_all, :], r.wd[:, cols]).astype(BF16)
            return carry2

        lax.fori_loop(0, width // 256, parts, 0)
        pair_copy(2, c).start()
        pair_copy(1, c).start()
        tick(2, c)

        @pl.when(c >= 1)
        def _():
            step_b(1, c - 1, send=False)

        return carry

    lax.fori_loop(0, chunks, phase_two, 0)
    late_tick(2, 0)
    step_b(1, chunks - 1, send=False)

    def send_glu(c, carry):
        across_copy(1, c).start()
        return carry

    lax.fori_loop(0, chunks, send_glu, 0)

    def transposed(src, i, dst):
        def piece(k, carry):
            rows = pl.ds(mult(k * 256, 256), 256)
            tile = src[rows, pl.ds(mult(i * 256, 256), 256)].T
            dst[k // 4, :, pl.ds(mult((k % 4) * 256, 256), 256)] = tile
            return carry

        lax.fori_loop(0, tokens // 256, piece, 0)

    def grad_of(turned, right, cols):
        total = None
        for k in range(2):
            rows = pl.ds(k * (tokens // 2), tokens // 2)
            operand = right[k, :, cols] if len(right.shape) == 3 else right[rows, cols]
            term = dot_nn(turned[k], operand)
            total = term if total is None else total + term
        return total.astype(BF16)

    def beside_copy(grads, arrivals, sems, g):
        block = 2 * g + 1 - parity
        send, recv = sems
        return remote(
            grads(pl.ds(mult(block * block_rows, block_rows), block_rows)),
            arrivals(pl.ds(mult(g * block_rows, block_rows), block_rows)),
            send.at[g],
            recv.at[g],
            beside,
        )

    def line_copy(grads, arrivals, sems, g):
        block = 2 * g + parity
        send, recv = sems
        return remote(
            grads(pl.ds(mult(block * block_rows, block_rows), block_rows)),
            arrivals(line),
            send.at[g],
            recv.at[line],
            (block, mp),
        )

    def glu_rows(rows):
        return r.grad_g.at[:, rows]

    def glu_beside(rows):
        return r.xg_h.at[:, rows]

    def glu_line(slot):
        return r.zg_h.at[slot]

    def att_rows(rows):
        return r.d_right.at[:, rows, pl.ds(0, wide)]

    def att_beside(rows):
        return r.xa_h.at[:, rows]

    def att_line(slot):
        return r.za_h.at[slot]

    glu_x = (glu_rows, glu_beside, (r.sem_xgs, r.sem_xgr))
    glu_z = (glu_rows, glu_line, (r.sem_zgs, r.sem_zgr))
    att_x = (att_rows, att_beside, (r.sem_xas, r.sem_xar))
    att_z = (att_rows, att_line, (r.sem_zas, r.sem_zar))

    def each(count, act):
        def one(j, carry):
            act(j)
            return carry

        if count == 1:
            act(0)
        else:
            lax.fori_loop(0, count, one, 0)

    def glu_group(i, carry):
        rows = pl.ds(mult(i * 256, 256), 256)
        transposed(r.n2, i, r.part)

        def sides(t, carry2):
            cols = pl.ds(mult(t * 256, 256), 256)
            r.grad_g[0, rows, cols] = grad_of(r.part, r.d_left, cols)
            r.grad_g[1, rows, cols] = grad_of(r.part, r.d_right, cols)
            return carry2

        lax.fori_loop(0, fp // 256, sides, 0)
        transposed(r.cot, i, r.part_g)

        def down(t, carry2):
            cols = pl.ds(mult(t * 256, 256), 256)
            r.grad_g[2, rows, cols] = grad_of(r.part_g, r.mixed, cols)
            return carry2

        lax.fori_loop(0, fp // 256, down, 0)
        each(per_group, lambda j: beside_copy(*glu_x, i * per_group + j).start())
        return carry

    lax.fori_loop(0, groups, glu_group, 0)

    def line_step(kinds, lanes, x, z, arrivals_h, stage, grads, g):
        copy = beside_copy(*x, g)
        copy.wait_recv()
        copy.wait_send()
        here = pl.ds(mult(g * block_rows, block_rows), block_rows)
        loads = []
        for t in range(kinds):
            load = pltpu.make_async_copy(
                arrivals_h.at[t, here],
                stage.at[pl.ds(t * block_rows, block_rows), pl.ds(0, lanes)],
                r.sem_stage.at[t],
            )
            load.start()
            loads.append(load)
        for load in loads:
            load.wait()
        step = min(16, block_rows)
        cols = pl.ds(0, lanes)

        for t in range(kinds):

            def piece(i, carry):
                sub = mult(i * step, step)
                there = pl.ds(mult((2 * g + parity) * block_rows + sub, step), step)
                mine = grads[t, there, cols].astype(F32)
                theirs = stage[pl.ds(mult(t * block_rows + sub, step), step), cols].astype(F32)
                grads[t, there, cols] = (mine + theirs).astype(BF16)
                return carry

            lax.fori_loop(0, block_rows // step, piece, 0)

        @pl.when(g != line)
        def _():
            line_copy(*z, g).start()

    def glu_line_step(g):
        line_step(3, fp, glu_x, glu_z, r.xg_h, r.mixed, r.grad_g, g)

    def att_line_step(g):
        line_step(2, wide, att_x, att_z, r.xa_h, r.d_left, r.d_right, g)

    def phase_three(c, carry):
        for n in range(2):

            @pl.when(c == n)
            def _():
                late_tick(2, n + 1)

        step_e(2, c)
        rows_all = pl.ds(base(c), CHUNK)
        r.gate_now[...] = dot_nt(r.do[rows_all, :], r.wo[...])

        def attend_back(i, carry2):
            tile, rows, lanes = tile_of(c, i)
            near = pl.ds(mult((i // head_pairs) * TILE, TILE), TILE)
            here = pl.ds(lanes, TILE)
            d_gated = r.gate_now[near, here]
            sigma = jax.nn.sigmoid(r.gate[rows, here].astype(F32))
            attended = r.attended[rows, here].astype(F32)
            factor = lax.rsqrt(head_mean(attended * attended) + EPS)
            head_normed = attended * factor
            d_head = d_gated * sigma
            d_gate = d_head * head_normed * (1.0 - sigma)
            r.d_all[rows, pl.ds(3 * wc + lanes, TILE)] = d_gate.astype(BF16)
            d_att = factor * (d_head - head_normed * head_mean(d_head * head_normed))
            d_stack = stacked(d_att.astype(BF16))
            probs, stack, keys = probs_of(tile, rows, lanes)
            values = r.qkv[rows, pl.ds(2 * wc + lanes, TILE)]
            d_probs = dot_nt(d_stack, values)
            d_values = dot_tn(probs.astype(BF16), d_stack)
            r.d_all[rows, pl.ds(2 * wc + lanes, TILE)] = d_values.astype(BF16)
            delta = jnp.sum(probs * d_probs, axis=-1, keepdims=True)
            d_scores = (probs * (d_probs - delta)).astype(BF16)
            d_queries = unstacked(dot_nn(d_scores, keys)) * HD ** (-0.5)
            r.d_all[rows, here] = d_queries.astype(BF16)
            d_keys = dot_tn(d_scores, stack) * HD ** (-0.5)
            r.d_all[rows, pl.ds(wc + lanes, TILE)] = d_keys.astype(BF16)
            return carry2

        lax.fori_loop(0, tiles * head_pairs, attend_back, 0)

        def back_piece(t, carry2):
            cols = pl.ds(mult(t * 256, 256), 256)
            r.part[c % 2, :, cols] = dot_nt(r.d_all[rows_all, :], r.w[cols, :]).astype(BF16)
            return carry2

        lax.fori_loop(0, width // 256, back_piece, 0)
        pair_copy(3, c).start()
        tick(3, c)

        for i in range(groups):

            @pl.when(c == 2 * i + 1)
            def _():
                each(per_group, lambda j: glu_line_step(i * per_group + j))

        return carry

    lax.fori_loop(0, chunks, phase_three, 0)
    late_tick(3, 0)

    def att_group(i, carry):
        rows = pl.ds(mult(i * 256, 256), 256)
        transposed(r.n1, i, r.part_g)

        def store(t, total):
            for u in range(wc // 128):
                at_col = t * (wc // 128) + u
                cols = pl.ds(mult((at_col % (wide // 128)) * 128, 128), 128)
                r.d_right[at_col // (wide // 128), rows, cols] = total[:, u * 128 : u * 128 + 128]

        def four(t, carry2):
            store(t, grad_of(r.part_g, r.d_all, pl.ds(mult(t * wc, wc), wc)))
            return carry2

        lax.fori_loop(0, 4, four, 0)
        transposed(r.do, i, r.part_g)
        store(4, grad_of(r.part_g, r.gated, pl.ds(0, wc)))
        each(per_group, lambda j: beside_copy(*att_x, i * per_group + j).start())
        for n in range(2):

            @pl.when(i == n)
            def _():
                late_tick(3, n + 1)

        return carry

    lax.fori_loop(0, groups, att_group, 0)

    def glu_result(c, carry):
        step_c(1, c)
        return carry

    lax.fori_loop(0, chunks, glu_result, 0)

    def att_lines(g, carry):
        att_line_step(g)
        return carry

    lax.fori_loop(0, pairs, att_lines, 0)

    def glu_forward(c, carry):
        step_d(1, c)
        return carry

    lax.fori_loop(0, chunks, glu_forward, 0)

    def finish(kinds, lanes, z, arrivals_h, stage, grads, out):
        cols = pl.ds(0, lanes)

        def arrived(j, carry):
            @pl.when(j != line)
            def _():
                block = 2 * j + parity
                remote(
                    z[0](pl.ds(mult(dp * block_rows, block_rows), block_rows)),
                    z[1](j),
                    z[2][0].at[j],
                    z[2][1].at[j],
                    (block, mp),
                ).wait_recv()
                line_copy(*z, j).wait_send()

            return carry

        lax.fori_loop(0, pairs, arrived, 0)
        for t in range(kinds):

            def fetch(j):
                return pltpu.make_async_copy(
                    arrivals_h.at[j, t],
                    stage.at[pl.ds(mult(j * block_rows, block_rows), block_rows), cols],
                    r.sem_stage.at[t],
                )

            def get(j, carry):
                @pl.when(j != line)
                def _():
                    fetch(j).start()
                    fetch(j).wait()

                return carry

            lax.fori_loop(0, pairs, get, 0)
            step = min(16, block_rows)

            def piece(i, carry):
                sub = mult(i * step, step)
                total = grads[t, pl.ds(mult(dp * block_rows + sub, step), step), cols].astype(F32)
                for j in range(pairs):
                    term = stage[pl.ds(mult(j * block_rows + sub, step), step), cols].astype(F32)
                    total = total + jnp.where(j == line, 0.0, term)
                out[t, pl.ds(sub, step), :] = total
                return carry

            lax.fori_loop(0, block_rows // step, piece, 0)

    finish(3, fp, glu_z, r.zg_h, r.mixed, r.grad_g, r.out_g)
    finish(2, wide, att_z, r.za_h, r.d_left, r.d_right, r.out_a)

    def ends(c, carry):
        step_e(1, c)
        step_e(3, c)
        return carry

    lax.fori_loop(0, chunks, ends, 0)


def fused(ndp, args):
    tokens, seg, wq, wk, wv, wg, wo, wl, wr, wd, cot = args
    rows, width = tokens.shape
    wc, ff = wq.shape[1], wl.shape[1]
    fp = (ff + 255) // 256 * 256
    chunks = rows // CHUNK
    quarter = CHUNK // 4
    own = rows // 4
    br = width // ndp
    pairs = ndp // 2
    wide = 5 * wc // 2
    hbm = pl.BlockSpec(memory_space=pl.ANY)
    vmem = pl.BlockSpec(memory_space=pltpu.VMEM)
    ins = [
        ("tok_h", tokens, hbm),
        ("seg", seg.reshape(rows // TILE, TILE), vmem),
        ("wq_h", wq, hbm),
        ("wk_h", wk, hbm),
        ("wv_h", wv, hbm),
        ("wg_h", wg, hbm),
        ("wo_h", wo, hbm),
        ("wl_h", wl, hbm),
        ("wr_h", wr, hbm),
        ("wd_h", wd, hbm),
        ("cot_h", cot, hbm),
    ]
    outs = [
        ("out_h", (rows, width), BF16, hbm),
        ("gt_h", (rows, width), BF16, hbm),
        ("out_g", (3, br, fp), F32, vmem),
        ("out_a", (2, br, wide), F32, vmem),
        ("xg_h", (3, pairs * br, fp), BF16, hbm),
        ("xa_h", (2, pairs * br, wide), BF16, hbm),
        ("zg_h", (pairs, 3, br, fp), BF16, hbm),
        ("za_h", (pairs, 2, br, wide), BF16, hbm),
    ]
    dma = pltpu.SemaphoreType.DMA
    scratch = [
        ("n1", pltpu.VMEM((rows, width), BF16)),
        ("tok_own", pltpu.VMEM((own, width), BF16)),
        ("cot", pltpu.VMEM((rows, width), BF16)),
        ("w", pltpu.VMEM((width, 4 * wc), BF16)),
        ("wo", pltpu.VMEM((wc, width), BF16)),
        ("wl", pltpu.VMEM((width, fp), BF16)),
        ("wr", pltpu.VMEM((width, fp), BF16)),
        ("wd", pltpu.VMEM((fp, width), BF16)),
        ("stage", pltpu.VMEM((width // 2, ff), BF16)),
        ("qkv", pltpu.VMEM((rows, 3 * wc), BF16)),
        ("gate", pltpu.VMEM((rows, wc), BF16)),
        ("gate_now", pltpu.VMEM((CHUNK, wc), F32)),
        ("attended", pltpu.VMEM((rows, wc), BF16)),
        ("gated", pltpu.VMEM((rows, wc), BF16)),
        ("n2", pltpu.VMEM((rows, width), BF16)),
        ("mixed", pltpu.VMEM((rows, fp), BF16)),
        ("d_left", pltpu.VMEM((rows, fp), BF16)),
        ("d_right", pltpu.VMEM((2, rows // 2, fp), BF16)),
        ("do", pltpu.VMEM((rows, width), BF16)),
        ("part", pltpu.VMEM((2, CHUNK, width), BF16)),
        ("part_g", pltpu.VMEM((2, CHUNK, width), BF16)),
        ("pair", pltpu.VMEM((RING, CHUNK // 2, width), BF16)),
        ("pair_g", pltpu.VMEM((RING, CHUNK // 2, width), BF16)),
        ("sent", pltpu.VMEM((own, width), BF16)),
        ("sent_g", pltpu.VMEM((own, width), BF16)),
        ("got", pltpu.VMEM((own, width), BF16)),
        ("got_g", pltpu.VMEM((own, width), BF16)),
        ("own", pltpu.VMEM((2, quarter, width), F32)),
        ("own_g", pltpu.VMEM((own, width), BF16)),
        ("hidden", pltpu.VMEM((own, width), F32)),
        ("d_hidden", pltpu.VMEM((own, width), F32)),
        ("grad_g", pltpu.VMEM((3, width, fp), BF16)),
        ("sem_tok", dma((chunks,))),
        ("sem_w", dma((8,))),
        ("sem_stage", dma((5,))),
    ]
    for name in ("as", "ar", "bs", "br", "cs", "cr", "ps", "pr", "ds", "dr"):
        scratch.append(("sem_" + name, dma((4 * chunks,))))
    scratch.append(("sem_o", dma((2 * chunks,))))
    for name in ("xgs", "xgr", "zgs", "zgr", "xas", "xar", "zas", "zar"):
        scratch.append(("sem_" + name, dma((pairs,))))
    names = [n for n, *_ in ins] + [n for n, *_ in outs] + [n for n, _ in scratch]

    def call(*refs):
        named = dict(zip(names, refs))
        named["d_all"] = named["n2"]
        kernel(list(named), ndp, *named.values())

    flops = 6 * rows * width * (5 * wc + 3 * ff)
    result = pl.pallas_call(
        call,
        out_shape=[jax.ShapeDtypeStruct(s, d) for _, s, d, _ in outs],
        in_specs=[s for *_, s in ins],
        out_specs=[s for *_, s in outs],
        scratch_shapes=[s for _, s in scratch],
        compiler_params=pltpu.CompilerParams(
            collective_id=0, has_side_effects=True, vmem_limit_bytes=67043328
        ),
        cost_estimate=pl.CostEstimate(flops=flops, bytes_accessed=1 << 25, transcendentals=1 << 22),
        name="fused_layer",
    )(*[a for _, a, _ in ins])
    return result[:4]


def body(ndp, *args):
    out, grad_tokens, glu, att = fused(ndp, args)
    ff, wc = args[7].shape[1], args[2].shape[1]
    att = jnp.concatenate([att[0], att[1]], axis=1)
    return (
        out,
        grad_tokens,
        att[:, :wc],
        att[:, wc : 2 * wc],
        att[:, 2 * wc : 3 * wc],
        att[:, 3 * wc : 4 * wc],
        att[:, 4 * wc :].T,
        glu[0, :, :ff],
        glu[1, :, :ff],
        glu[2, :, :ff].T,
    )


def solution(mesh):
    rows, cols, down = P("dp", None), P(None, "mp"), P("mp", None)
    grad = P("dp", "mp")
    return jax.shard_map(
        functools.partial(body, mesh.shape["dp"]),
        mesh=mesh,
        in_specs=(rows, rows, cols, cols, cols, cols, down, cols, cols, down, rows),
        out_specs=(rows, rows, grad, grad, grad, grad, P("mp", "dp"), grad, grad, P("mp", "dp")),
        check_vma=False,
    )
```

time: 705 us -> 273 us (0.39)
  waiting for transfers between devices: 421 us -> 0 us
  Pallas kernels: 0 us -> 252 us
  matrix products: 116 us -> 0 us
  local copies, waits for them, and re-layouts: 89 us -> 15.8 us
  other arithmetic: 54.2 us -> 0.8 us
  between operations: 14.7 us -> 0.68 us
    psum x3 -> x0, waiting for transfers between devices: 272 us -> none  [head_total(): lax.psum(partial_value.astype(jnp.bfloat16), 'mp').astype(jnp.float32)]
    pallas_call x0 -> x1, Pallas kernels: none -> 252 us  [fused(): pl.pallas_call(call, out_shape=[jax.ShapeDtypeStruct(s, d) for _, s, d, _...]
    unnamed x7 -> x0, waiting for transfers between devices: 149 us -> none
    dot_general x30 -> x0, matrix products: 116 us -> none  [the longest x1 9.88 us: body(): jnp.einsum('tc,dc->td', d_gate, w_gate, preferred_element_type=jnp.float32)]
    reshape x7 -> x0, local copies, waits for them, and re-layouts: 26.5 us -> none  [the longest x2 8.58 us: body(): query_blocks = queries.reshape(blocks, BLOCK, heads_here, HD)]
    convert_element_type x8 -> x0, other arithmetic: 21.6 us -> none  [the longest x1 9.57 us: body(): grad_tokens = d_source.astype(jnp.bfloat16)]
    reduce_sum x5 -> x0, other arithmetic: 20.6 us -> none  [the longest x2 11.1 us: norm_back(): jnp.mean(grad * normed, axis=-1, keepdims=True)]
    convert_element_type x6 -> x0, local copies, waits for them, and re-layouts: 20.3 us -> none  [the longest x2 10.1 us: body(): d_queries = d_queries.reshape(rows_all, width_c).astype(jnp.bfloat16)]
  transfers between devices with their start and end apart: 5 -> 0, of which waited for: 5 -> 0; matrix products, arithmetic and copies ran while one was open for 10% -> 0% of each run, Pallas kernels for 0% -> 0%
where the time goes in v2:
time: 273 us; the launch traced here: 270 us
  Pallas kernels  252 us (92%)
  local copies, waits for them, and re-layouts  15.8 us (6%)
    pallas_call x1, Pallas kernels, fused(): pl.pallas_call(call, out_shape=[jax.ShapeDtypeStruct(s, d) for _, s, d, _...  252 us
    unnamed x14, local copies, waits for them, and re-layouts  14.5 us

profile of v2, /device:TPU:9, one launch (start us, length us, event | category | flops | bytes accessed | tf_op | source)
XLA Modules:
  0.0 269.8 jit_solution(9517069387404256063)
XLA Ops:
  0.6 0.0 copy-start.1
  0.7 2.7 copy.21.refs_7_
  3.3 0.0 copy-done.1
  3.3 1.6 copy.22.refs_8_
  4.9 252.5 %fused_layer.1 = (bf16[2048,1024]{1,0:T(8,128)(2,1)}, bf16[2048,1024]{1,0:T(8,128)(2,1)}, f32[3,128,768]{2,1,0:T(8,128)}, f32[2,128,640]{2,1,0:T(8,128)}, bf16[3...) custom-call(bf16[2048,1024]{1,0:T(8,128)(2,1)} %refs_0_.1, ...), custom_call_target="tpu_custom_call" | custom-call | flops 42681237504 | bytes 33554432 | tf_op jit(solution)/shard_map/fused_layer/pallas_call | solution.py:890
  257.3 0.0 copy-start.2
  257.4 1.2 slice_bitcast_fusion.3
  258.6 0.8 slice_bitcast_fusion.5
  259.4 0.8 copy.23
  260.1 0.0 copy-done.2
  260.1 0.1 slice_bitcast_fusion
  260.2 0.9 copy.26
  261.1 0.9 copy.25
  262.0 0.9 copy.24
  262.9 0.0 copy-start
  262.9 4.8 %copy.29 = bf16[2048,1024]{1,0:T(8,128)(2,1)} copy(bf16[2048,1024]{1,0:T(8,128)(2,1)} %get-tuple-element.48) | data formatting | bytes 8388608
  267.8 0.0 copy-done
  267.8 2.0 copy.30
Async XLA Ops:
  0.6 2.7 copy-start.1
  257.3 2.8 %copy-start.2 = (f32[3,128,768]{2,1,0:T(8,128)S(1)}, f32[3,128,768]{2,1,0:T(8,128)}, u32[]{:S(2)}) copy-start(f32[3,128,768]{2,1,0:T(8,128)} %get-tuple-element.17) | copy-start | bytes 3538948
  262.9 4.8 %copy-start = (bf16[2048,1024]{1,0:T(8,128)(2,1)S(1)}, bf16[2048,1024]{1,0:T(8,128)(2,1)}, u32[]{:S(2)}) copy-start(bf16[2048,1024]{1,0:T(8,128)(2,1)} %get-tuple-element.49) | copy-start | bytes 12582916

commit v3 on v2

--- a/solution.py
+++ b/solution.py
@@ -53,9 +53,8 @@
     tokens, width = r.n1.shape
     chunks = tokens // CHUNK
     half, quarter = CHUNK // 2, CHUNK // 4
-    wc = r.wo.shape[0]
-    fp = r.wl.shape[1]
-    ff = r.wl_h.shape[1]
+    wc = r.wo_h.shape[0]
+    fp, ff = r.wl.shape[0], r.wl_h.shape[0]
     block_rows = width // ndp
     pairs = ndp // 2
     groups = width // 256
@@ -98,15 +97,27 @@
 
     lax.fori_loop(0, pairs, greet, 0)
 
+    pair_mp = mp + 1 - 2 * core
+    across_mp = mp + 2 - 4 * side
+
+    def group_of(who):
+        return pl.ds(mult(who * wc, wc), wc)
+
+    def wo_across():
+        there = r.wof.at[group_of(mp)]
+        return remote(r.wo_h, there, r.sem_wos.at[0], r.sem_wor.at[0], across)
+
+    def wo_partner():
+        there = r.wof.at[group_of(mp)]
+        return remote(r.wo_h, there, r.sem_wos.at[1], r.sem_wor.at[1], partner)
+
+    def wo_forward():
+        here = r.wof.at[group_of(across_mp)]
+        return remote(here, here, r.sem_wos.at[2], r.sem_wor.at[2], partner)
+
     def load_tokens(c):
         rows = pl.ds(mult(c * CHUNK, CHUNK), CHUNK)
         return pltpu.make_async_copy(r.tok_h.at[rows], r.n1.at[rows], r.sem_tok.at[c])
-
-    def load_stage(i):
-        src = r.wl_h if i < 2 else r.wr_h
-        return pltpu.make_async_copy(
-            src.at[pl.ds((i % 2) * (width // 2), width // 2)], r.stage, r.sem_w.at[7]
-        )
 
     load_tokens(0).start()
     w_loads = [
@@ -115,21 +126,31 @@
     ]
     for copy in w_loads:
         copy.start()
-    wo_load = pltpu.make_async_copy(r.wo_h, r.wo, r.sem_w.at[4])
+    wo_load = pltpu.make_async_copy(
+        r.wo_h, r.wof.at[pl.ds(mult(mp * wc, wc), wc)], r.sem_w.at[4]
+    )
     wo_load.start()
     for c in range(1, chunks):
         load_tokens(c).start()
-    load_stage(0).start()
-    wd_load = pltpu.make_async_copy(r.wd_h, r.wd.at[pl.ds(0, ff)], r.sem_w.at[5])
-    wd_load.start()
-    cot_load = pltpu.make_async_copy(r.cot_h, r.cot, r.sem_w.at[6])
+    glu_loads = [
+        pltpu.make_async_copy(h, v.at[pl.ds(0, ff)], r.sem_w.at[i])
+        for i, h, v in ((5, r.wd_h, r.wd), (6, r.wl_h, r.wl), (7, r.wr_h, r.wr))
+    ]
+    for copy in glu_loads:
+        copy.start()
+    cot_load = pltpu.make_async_copy(r.cot_h, r.cot, r.sem_w.at[8])
     cot_load.start()
 
     pl.semaphore_wait(barrier, 3 + pairs - 1)
+    for copy in (wo_across(), wo_partner()):
+        copy.start()
 
     def base(c):
         return mult(c * CHUNK, CHUNK)
 
+    def half_rows(c):
+        return pl.ds(mult(c * CHUNK + core * half, half), half)
+
     def own_rows(c):
         return pl.ds(mult(c * CHUNK + core * half + side * quarter, quarter), quarter)
 
@@ -158,7 +179,7 @@
         return r.got_g if s == 1 else r.got
 
     def full_of(s):
-        return (r.n2, r.out_h, r.do, r.gt_h)[s]
+        return (None, r.out_h, r.do, r.gt_h)[s]
 
     def at(s, c):
         return s * chunks + c
@@ -183,7 +204,7 @@
         )
 
     def result_src(s, c):
-        if s in (0, 2):
+        if s == 2:
             return full_of(s).at[own_rows(c)]
         return sent_of(s).at[kept(c)]
 
@@ -241,7 +262,7 @@
                 r.own[slot, pl.ds(rows, 32), :] = total
             return carry
 
-        lax.fori_loop(0, quarter // 32, piece, 0)
+        lax.fori_loop(0, quarter // 32, piece, 0, unroll=True)
         if send:
             across_copy(s, c).start()
 
@@ -260,11 +281,7 @@
                 total = r.own_g[mine, :].astype(F32) + arrived
             else:
                 total = r.own[slot, pl.ds(rows, 32), :] + arrived
-            if s == 0:
-                hidden = r.tok_own[mine, :].astype(F32) + total
-                r.hidden[mine, :] = hidden
-                r.n2[full, :] = (hidden * rms_factor(hidden)).astype(BF16)
-            elif s == 1:
+            if s == 1:
                 r.sent_g[mine, :] = (r.hidden[mine, :] + total).astype(BF16)
             elif s == 2:
                 hidden = r.hidden[mine, :]
@@ -273,13 +290,14 @@
                 r.d_hidden[mine, :] = d_hidden
                 r.do[full, :] = d_hidden.astype(BF16)
             else:
-                source = r.tok_own[mine, :].astype(F32)
+                held = pl.ds(mult(c * half + side * quarter + rows, 32), 32)
+                source = r.tok_half[held, :].astype(F32)
                 factor = rms_factor(source)
                 d_source = r.d_hidden[mine, :] + norm_back(total, source * factor, factor)
                 r.sent[mine, :] = d_source.astype(BF16)
             return carry
 
-        lax.fori_loop(0, quarter // 32, piece, 0)
+        lax.fori_loop(0, quarter // 32, piece, 0, unroll=True)
         result_across(s, c).start()
         result_partner(s, c).start()
         if s in (1, 3):
@@ -330,6 +348,57 @@
             step_c(s, chunks - 2 + n)
         step_d(s, chunks - 3 + n)
 
+    def gated_across(c):
+        here = r.do.at[pl.ds(base(c), CHUNK), group_of(mp)]
+        return remote(here, here, r.sem_bs.at[c], r.sem_br.at[c], across)
+
+    def gated_partner(c):
+        here = r.do.at[pl.ds(base(c), CHUNK), group_of(mp)]
+        return remote(here, here, r.sem_as.at[c], r.sem_ar.at[c], partner)
+
+    def gated_forward(c):
+        here = r.do.at[pl.ds(base(c), CHUNK), group_of(across_mp)]
+        return remote(here, here, r.sem_ds.at[c], r.sem_dr.at[c], partner)
+
+    def n2_partner(c):
+        here = r.n2.at[half_rows(c)]
+        return remote(here, here, r.sem_ps.at[c], r.sem_pr.at[c], partner)
+
+    def gated_pass(c):
+        gated_across(c).wait_recv()
+        gated_forward(c).start()
+
+    def gated_project(c):
+        gated_partner(c).wait_recv()
+        gated_forward(c).wait_recv()
+        rows = half_rows(c)
+        for t in range(width // 256):
+            cols = pl.ds(t * 256, 256)
+            total = dot_nn(r.do[rows, :], r.wof[:, cols])
+            r.own[0, :, cols] = total[:quarter]
+            r.own[1, :, cols] = total[quarter:]
+
+        def piece(i, carry):
+            q, sub = i // 2, mult((i % 2) * 32, 32)
+            held = pl.ds(mult(c * half + i * 32, 32), 32)
+            full = pl.ds(mult(c * CHUNK + core * half + i * 32, 32), 32)
+            hidden = r.tok_half[held, :].astype(F32) + r.own[q, pl.ds(sub, 32), :]
+            r.n2[full, :] = (hidden * rms_factor(hidden)).astype(BF16)
+
+            @pl.when(q == side)
+            def _():
+                r.hidden[pl.ds(mult(c * quarter + sub, 32), 32), :] = hidden
+
+            return carry
+
+        lax.fori_loop(0, half // 32, piece, 0, unroll=True)
+        n2_partner(c).start()
+
+    def gated_end(c):
+        n2_partner(c).wait_recv()
+        for copy in (gated_across(c), gated_partner(c), gated_forward(c), n2_partner(c)):
+            copy.wait_send()
+
     lane = lax.broadcasted_iota(jnp.int32, (TILE, TILE), 1)
     row = lax.broadcasted_iota(jnp.int32, (TILE, TILE), 0)
     first = lane < HD
@@ -374,12 +443,11 @@
 
     for copy in w_loads:
         copy.wait()
-    wo_load.wait()
 
     def phase_one(c, carry):
         rows_all = pl.ds(base(c), CHUNK)
         load_tokens(c).wait()
-        r.tok_own[kept(c), :] = r.n1[own_rows(c), :]
+        r.tok_half[pl.ds(mult(c * half, half), half), :] = r.n1[half_rows(c), :]
 
         def norm_piece(i, carry2):
             rows = pl.ds(mult(c * CHUNK + i * 32, 32), 32)
@@ -394,7 +462,7 @@
             r.qkv[rows_all, cols] = dot_nn(r.n1[rows_all, :], r.w[:, cols]).astype(BF16)
             return carry2
 
-        lax.fori_loop(0, 3, project, 0)
+        lax.fori_loop(0, 3, project, 0, unroll=True)
         r.gate_now[...] = dot_nn(r.n1[rows_all, :], r.w[:, pl.ds(3 * wc, wc)])
         r.gate[rows_all, :] = r.gate_now[...].astype(BF16)
 
@@ -407,74 +475,82 @@
             factor = lax.rsqrt(head_mean(attended * attended) + EPS)
             near = pl.ds(mult((i // head_pairs) * TILE, TILE), TILE)
             sigma = jax.nn.sigmoid(r.gate_now[near, pl.ds(lanes, TILE)])
-            r.gated[rows, pl.ds(lanes, TILE)] = (attended * factor * sigma).astype(BF16)
+            gated = (attended * factor * sigma).astype(BF16)
+            r.gated[rows, pl.ds(lanes, TILE)] = gated
+            r.do[rows, pl.ds(mult(mp * wc + lanes, TILE), TILE)] = gated
             return carry2
 
-        lax.fori_loop(0, tiles * head_pairs, attend, 0)
-
-        def out_piece(t, carry2):
-            cols = pl.ds(mult(t * 256, 256), 256)
-            r.part[c % 2, :, cols] = dot_nn(r.gated[rows_all, :], r.wo[:, cols]).astype(BF16)
-            return carry2
-
-        lax.fori_loop(0, width // 256, out_piece, 0)
-        pair_copy(0, c).start()
-
-        for i in range(4):
-
-            @pl.when(c == i)
-            def _():
-                load_stage(i).wait()
-                dst = r.wl if i < 2 else r.wr
-                start = (i % 2) * (width // 2)
-                for k in range(4):
-                    rows = pl.ds(start + k * (width // 8), width // 8)
-                    dst[rows, pl.ds(fp - 128, 128)] = jnp.zeros((width // 8, 128), BF16)
-                    dst[rows, pl.ds(0, ff)] = r.stage[pl.ds(k * (width // 8), width // 8), :]
-                if i < 3:
-                    load_stage(i + 1).start()
-
-        tick(0, c)
+        lax.fori_loop(0, tiles * head_pairs, attend, 0, unroll=True)
+
+        gated_across(c).start()
+        gated_partner(c).start()
+
+        @pl.when(c == 1)
+        def _():
+            wo_across().wait_recv()
+            wo_forward().start()
+
+        @pl.when(c >= 1)
+        def _():
+            gated_pass(c - 1)
+
+        @pl.when(c == 2)
+        def _():
+            wo_load.wait()
+            wo_partner().wait_recv()
+            wo_forward().wait_recv()
+            for copy in (wo_across(), wo_partner(), wo_forward()):
+                copy.wait_send()
+
+        @pl.when(c >= 2)
+        def _():
+            gated_project(c - 2)
+
         return carry
 
     lax.fori_loop(0, chunks, phase_one, 0)
 
-    wd_load.wait()
-    r.wd[pl.ds(ff, fp - ff), :] = jnp.zeros((fp - ff, width), BF16)
+    for copy in glu_loads:
+        copy.wait()
+    for weights in (r.wd, r.wl, r.wr):
+        weights[pl.ds(ff, fp - ff), :] = jnp.zeros((fp - ff, width), BF16)
     cot_load.wait()
 
     def phase_two(c, carry):
-        for n in range(3):
-
-            @pl.when(c == n)
-            def _():
-                late_tick(0, n)
-
-        step_e(0, c)
+        @pl.when(c == 0)
+        def _():
+            gated_pass(chunks - 1)
+            gated_project(chunks - 2)
+
+        @pl.when(c == 1)
+        def _():
+            gated_project(chunks - 1)
+
+        gated_end(c)
         rows_all = pl.ds(base(c), CHUNK)
         rows_half = pl.ds(mult((c % half_chunks) * CHUNK, CHUNK), CHUNK)
 
         def hidden_units(t, carry2):
             cols = pl.ds(mult(t * 256, 256), 256)
-            left = dot_nn(r.n2[rows_all, :], r.wl[:, cols])
-            right = dot_nn(r.n2[rows_all, :], r.wr[:, cols])
+            left = dot_nt(r.n2[rows_all, :], r.wl[cols, :])
+            right = dot_nt(r.n2[rows_all, :], r.wr[cols, :])
             r.mixed[rows_all, cols] = (left * right).astype(BF16)
             d_mixed = dot_nt(r.cot[rows_all, :], r.wd[cols, :])
             r.d_left[rows_all, cols] = (d_mixed * right).astype(BF16)
             r.d_right[c // half_chunks, rows_half, cols] = (d_mixed * left).astype(BF16)
             return carry2
 
-        lax.fori_loop(0, fp // 256, hidden_units, 0)
+        lax.fori_loop(0, fp // 256, hidden_units, 0, unroll=True)
 
         def parts(t, carry2):
             cols = pl.ds(mult(t * 256, 256), 256)
-            back = dot_nt(r.d_left[rows_all, :], r.wl[cols, :])
-            back = back + dot_nt(r.d_right[c // half_chunks, rows_half, :], r.wr[cols, :])
+            back = dot_nn(r.d_left[rows_all, :], r.wl[:, cols])
+            back = back + dot_nn(r.d_right[c // half_chunks, rows_half, :], r.wr[:, cols])
             r.part[c % 2, :, cols] = back.astype(BF16)
             r.part_g[c % 2, :, cols] = dot_nn(r.mixed[rows_all, :], r.wd[:, cols]).astype(BF16)
             return carry2
 
-        lax.fori_loop(0, width // 256, parts, 0)
+        lax.fori_loop(0, width // 256, parts, 0, unroll=True)
         pair_copy(2, c).start()
         pair_copy(1, c).start()
         tick(2, c)
@@ -578,7 +654,7 @@
             r.grad_g[1, rows, cols] = grad_of(r.part, r.d_right, cols)
             return carry2
 
-        lax.fori_loop(0, fp // 256, sides, 0)
+        lax.fori_loop(0, fp // 256, sides, 0, unroll=True)
         transposed(r.cot, i, r.part_g)
 
         def down(t, carry2):
@@ -586,7 +662,7 @@
             r.grad_g[2, rows, cols] = grad_of(r.part_g, r.mixed, cols)
             return carry2
 
-        lax.fori_loop(0, fp // 256, down, 0)
+        lax.fori_loop(0, fp // 256, down, 0, unroll=True)
         each(per_group, lambda j: beside_copy(*glu_x, i * per_group + j).start())
         return carry
 
@@ -642,7 +718,7 @@
 
         step_e(2, c)
         rows_all = pl.ds(base(c), CHUNK)
-        r.gate_now[...] = dot_nt(r.do[rows_all, :], r.wo[...])
+        r.gate_now[...] = dot_nt(r.do[rows_all, :], r.wof[group_of(mp), :])
 
         def attend_back(i, carry2):
             tile, rows, lanes = tile_of(c, i)
@@ -671,14 +747,14 @@
             r.d_all[rows, pl.ds(wc + lanes, TILE)] = d_keys.astype(BF16)
             return carry2
 
-        lax.fori_loop(0, tiles * head_pairs, attend_back, 0)
+        lax.fori_loop(0, tiles * head_pairs, attend_back, 0, unroll=True)
 
         def back_piece(t, carry2):
             cols = pl.ds(mult(t * 256, 256), 256)
             r.part[c % 2, :, cols] = dot_nt(r.d_all[rows_all, :], r.w[cols, :]).astype(BF16)
             return carry2
 
-        lax.fori_loop(0, width // 256, back_piece, 0)
+        lax.fori_loop(0, width // 256, back_piece, 0, unroll=True)
         pair_copy(3, c).start()
         tick(3, c)
 
@@ -707,7 +783,7 @@
             store(t, grad_of(r.part_g, r.d_all, pl.ds(mult(t * wc, wc), wc)))
             return carry2
 
-        lax.fori_loop(0, 4, four, 0)
+        lax.fori_loop(0, 4, four, 0, unroll=True)
         transposed(r.do, i, r.part_g)
         store(4, grad_of(r.part_g, r.gated, pl.ds(0, wc)))
         each(per_group, lambda j: beside_copy(*att_x, i * per_group + j).start())
@@ -739,58 +815,27 @@
 
     lax.fori_loop(0, chunks, glu_forward, 0)
 
-    def finish(kinds, lanes, z, arrivals_h, stage, grads, out):
-        cols = pl.ds(0, lanes)
+    def settle(z, sem):
+        grads, arrivals, sems = z
+        here = pl.ds(mult(dp * block_rows, block_rows), block_rows)
+        mine = pltpu.make_async_copy(grads(here), arrivals(line), sem)
+        mine.start()
 
         def arrived(j, carry):
             @pl.when(j != line)
             def _():
-                block = 2 * j + parity
                 remote(
-                    z[0](pl.ds(mult(dp * block_rows, block_rows), block_rows)),
-                    z[1](j),
-                    z[2][0].at[j],
-                    z[2][1].at[j],
-                    (block, mp),
+                    grads(here), arrivals(j), sems[0].at[j], sems[1].at[j], (2 * j + parity, mp)
                 ).wait_recv()
                 line_copy(*z, j).wait_send()
 
             return carry
 
         lax.fori_loop(0, pairs, arrived, 0)
-        for t in range(kinds):
-
-            def fetch(j):
-                return pltpu.make_async_copy(
-                    arrivals_h.at[j, t],
-                    stage.at[pl.ds(mult(j * block_rows, block_rows), block_rows), cols],
-                    r.sem_stage.at[t],
-                )
-
-            def get(j, carry):
-                @pl.when(j != line)
-                def _():
-                    fetch(j).start()
-                    fetch(j).wait()
-
-                return carry
-
-            lax.fori_loop(0, pairs, get, 0)
-            step = min(16, block_rows)
-
-            def piece(i, carry):
-                sub = mult(i * step, step)
-                total = grads[t, pl.ds(mult(dp * block_rows + sub, step), step), cols].astype(F32)
-                for j in range(pairs):
-                    term = stage[pl.ds(mult(j * block_rows + sub, step), step), cols].astype(F32)
-                    total = total + jnp.where(j == line, 0.0, term)
-                out[t, pl.ds(sub, step), :] = total
-                return carry
-
-            lax.fori_loop(0, block_rows // step, piece, 0)
-
-    finish(3, fp, glu_z, r.zg_h, r.mixed, r.grad_g, r.out_g)
-    finish(2, wide, att_z, r.za_h, r.d_left, r.d_right, r.out_a)
+        mine.wait()
+
+    settle(glu_z, r.sem_stage.at[0])
+    settle(att_z, r.sem_stage.at[1])
 
     def ends(c, carry):
         step_e(1, c)
@@ -821,16 +866,14 @@
         ("wv_h", wv, hbm),
         ("wg_h", wg, hbm),
         ("wo_h", wo, hbm),
-        ("wl_h", wl, hbm),
-        ("wr_h", wr, hbm),
+        ("wl_h", wl.T, hbm),
+        ("wr_h", wr.T, hbm),
         ("wd_h", wd, hbm),
         ("cot_h", cot, hbm),
     ]
     outs = [
         ("out_h", (rows, width), BF16, hbm),
         ("gt_h", (rows, width), BF16, hbm),
-        ("out_g", (3, br, fp), F32, vmem),
-        ("out_a", (2, br, wide), F32, vmem),
         ("xg_h", (3, pairs * br, fp), BF16, hbm),
         ("xa_h", (2, pairs * br, wide), BF16, hbm),
         ("zg_h", (pairs, 3, br, fp), BF16, hbm),
@@ -839,14 +882,13 @@
     dma = pltpu.SemaphoreType.DMA
     scratch = [
         ("n1", pltpu.VMEM((rows, width), BF16)),
-        ("tok_own", pltpu.VMEM((own, width), BF16)),
+        ("tok_half", pltpu.VMEM((rows // 2, width), BF16)),
         ("cot", pltpu.VMEM((rows, width), BF16)),
         ("w", pltpu.VMEM((width, 4 * wc), BF16)),
-        ("wo", pltpu.VMEM((wc, width), BF16)),
-        ("wl", pltpu.VMEM((width, fp), BF16)),
-        ("wr", pltpu.VMEM((width, fp), BF16)),
+        ("wof", pltpu.VMEM((width, width), BF16)),
+        ("wl", pltpu.VMEM((fp, width), BF16)),
+        ("wr", pltpu.VMEM((fp, width), BF16)),
         ("wd", pltpu.VMEM((fp, width), BF16)),
-        ("stage", pltpu.VMEM((width // 2, ff), BF16)),
         ("qkv", pltpu.VMEM((rows, 3 * wc), BF16)),
         ("gate", pltpu.VMEM((rows, wc), BF16)),
         ("gate_now", pltpu.VMEM((CHUNK, wc), F32)),
@@ -871,11 +913,13 @@
         ("d_hidden", pltpu.VMEM((own, width), F32)),
         ("grad_g", pltpu.VMEM((3, width, fp), BF16)),
         ("sem_tok", dma((chunks,))),
-        ("sem_w", dma((8,))),
-        ("sem_stage", dma((5,))),
+        ("sem_w", dma((9,))),
+        ("sem_stage", dma((3 * pairs,))),
     ]
     for name in ("as", "ar", "bs", "br", "cs", "cr", "ps", "pr", "ds", "dr"):
         scratch.append(("sem_" + name, dma((4 * chunks,))))
+    scratch.append(("sem_wos", dma((3,))))
+    scratch.append(("sem_wor", dma((3,))))
     scratch.append(("sem_o", dma((2 * chunks,))))
     for name in ("xgs", "xgr", "zgs", "zgr", "xas", "xar", "zas", "zar"):
         scratch.append(("sem_" + name, dma((pairs,))))
@@ -899,25 +943,109 @@
         cost_estimate=pl.CostEstimate(flops=flops, bytes_accessed=1 << 25, transcendentals=1 << 22),
         name="fused_layer",
     )(*[a for _, a, _ in ins])
-    return result[:4]
+    return result[0], result[1], result[4], result[5]
+
+
+def collect(br, wc, ff, refs):
+    out_h, gt_h, zg_h, za_h = refs[:4]
+    out_o, gt_o, *grads_o = refs[4:14]
+    held, zg, za, sem_in, sem_out, sem_z, *grads = refs[14:]
+    pairs = zg.shape[0]
+    pieces = held.shape[1]
+    rows = held.shape[2]
+    loads = [
+        pltpu.make_async_copy(zg_h, zg, sem_z.at[0]),
+        pltpu.make_async_copy(za_h, za, sem_z.at[1]),
+    ]
+    moves = []
+    for i in range(pieces):
+        for k, (src, dst) in enumerate(((out_h, out_o), (gt_h, gt_o))):
+            span = pl.ds(i * rows, rows)
+            get = pltpu.make_async_copy(src.at[span], held.at[k, i], sem_in.at[k * pieces + i])
+            put = pltpu.make_async_copy(held.at[k, i], dst.at[span], sem_out.at[k * pieces + i])
+            moves.append((get, put))
+    for copy in loads:
+        copy.start()
+    for get, _ in moves:
+        get.start()
+    for copy in loads:
+        copy.wait()
+
+    def total(ref, t, cols):
+        value = ref[0, t, :, cols].astype(F32)
+        for j in range(1, pairs):
+            value = value + ref[j, t, :, cols].astype(F32)
+        return value
+
+    stores = [pltpu.make_async_copy(v, h, sem_z.at[2 + i]) for i, (v, h) in enumerate(zip(grads, grads_o))]
+    wide = za.shape[3]
+    todo = list(moves)
+
+    def pump():
+        if todo:
+            get, put = todo.pop(0)
+            get.wait()
+            put.start()
+
+    for kind in range(5):
+        for u in range(wc // 128):
+            at_col = kind * (wc // 128) + u
+            col = (at_col % (wide // 128)) * 128
+            value = total(za, at_col // (wide // 128), pl.ds(col, 128))
+            if kind < 4:
+                grads[kind][:, pl.ds(u * 128, 128)] = value
+            else:
+                grads[kind][pl.ds(u * 128, 128), :] = value.T
+        stores[kind].start()
+        pump()
+    for t in range(3):
+        for start in range(0, ff, 128):
+            size = min(128, ff - start)
+            value = total(zg, t, pl.ds(start, 128)).T
+            grads[5 + t][pl.ds(start, size), :] = value[:size]
+        stores[5 + t].start()
+        pump()
+    while todo:
+        pump()
+    for _, put in moves:
+        put.wait()
+    for copy in stores:
+        copy.wait()
+
+
+def collected(arrays, br, wc, ff):
+    rows, width = arrays[0].shape
+    pieces = 8
+    hbm = pl.BlockSpec(memory_space=pl.ANY)
+    dma = pltpu.SemaphoreType.DMA
+    shapes = [(br, wc)] * 4 + [(wc, br)] + [(ff, br)] * 3
+    outs = [((rows, width), BF16)] * 2 + [(s, F32) for s in shapes]
+    return pl.pallas_call(
+        lambda *refs: collect(br, wc, ff, refs),
+        out_shape=[jax.ShapeDtypeStruct(s, d) for s, d in outs],
+        in_specs=[hbm] * 4,
+        out_specs=[hbm] * 10,
+        scratch_shapes=[
+            pltpu.VMEM((2, pieces, rows // pieces, width), BF16),
+            pltpu.VMEM(arrays[2].shape, BF16),
+            pltpu.VMEM(arrays[3].shape, BF16),
+            dma((2 * pieces,)),
+            dma((2 * pieces,)),
+            dma((10,)),
+        ]
+        + [pltpu.VMEM(s, F32) for s in shapes],
+        compiler_params=pltpu.CompilerParams(vmem_limit_bytes=67043328),
+        name="collect",
+    )(*arrays)
 
 
 def body(ndp, *args):
-    out, grad_tokens, glu, att = fused(ndp, args)
-    ff, wc = args[7].shape[1], args[2].shape[1]
-    att = jnp.concatenate([att[0], att[1]], axis=1)
-    return (
-        out,
-        grad_tokens,
-        att[:, :wc],
-        att[:, wc : 2 * wc],
-        att[:, 2 * wc : 3 * wc],
-        att[:, 3 * wc : 4 * wc],
-        att[:, 4 * wc :].T,
-        glu[0, :, :ff],
-        glu[1, :, :ff],
-        glu[2, :, :ff].T,
+    arrays = fused(ndp, args)
+    ff, wc, width = args[7].shape[1], args[2].shape[1], args[0].shape[1]
+    out, grad_tokens, query, key, value, gate, proj, left, right, down = collected(
+        arrays, width // ndp, wc, ff
     )
+    return out, grad_tokens, query, key, value, gate, proj, left.T, right.T, down
 
 
 def solution(mesh):

time: 273 us -> 239 us (0.88)
  Pallas kernels: 252 us -> 234 us
  local copies, waits for them, and re-layouts: 15.8 us -> 0 us
    pallas_call x1, Pallas kernels: 252 us -> 225 us  [fused(): pl.pallas_call(call, out_shape=[jax.ShapeDtypeStruct(s, d) for _, s, d, _...]
    unnamed x14 -> x0, local copies, waits for them, and re-layouts: 14.5 us -> none
    pallas_call x0 -> x1, Pallas kernels: none -> 8.55 us  [collected(): pl.pallas_call(lambda *refs: collect(br, wc, ff, refs), out_shape=[jax.Sh...]
where the time goes in v3:
time: 239 us; the launch traced here: 235 us
  Pallas kernels  234 us (98%)
    pallas_call x1, Pallas kernels, fused(): pl.pallas_call(call, out_shape=[jax.ShapeDtypeStruct(s, d) for _, s, d, _...  225 us
    pallas_call x1, Pallas kernels, collected(): pl.pallas_call(lambda *refs: collect(br, wc, ff, refs), out_shape=[jax.Sh...  8.55 us

profile of v3, /device:TPU:9, one launch (start us, length us, event | category | flops | bytes accessed | tf_op | source)
XLA Modules:
  0.0 234.8 jit_solution(17492513862830117301)
XLA Ops:
  0.6 225.4 %fused_layer.1 = (bf16[2048,1024]{1,0:T(8,128)(2,1)}, bf16[2048,1024]{1,0:T(8,128)(2,1)}, bf16[3,512,768]{2,1,0:T(8,128)(2,1)}, bf16[2,512,640]{2,1,0:T(8,128)(2...) custom-call(bf16[2048,1024]{1,0:T(8,128)(2,1)} %refs_0_.1, s32[16,128]{1,0:T(8,128)} %bitcast.9, ...), custom_call_target="tpu_custom_call" | custom-call | flops 42681237504 | bytes 33554432 | tf_op jit(solution)/shard_map/fused_layer/pallas_call | solution.py:934
  226.0 8.6 %collect.1 = (bf16[2048,1024]{1,0:T(8,128)(2,1)}, bf16[2048,1024]{1,0:T(8,128)(2,1)}, f32[128,256]{1,0:T(8,128)}, f32[128,256]{1,0:T(8,128)}, f32[128,256]{1,0:T...) custom-call(bf16[2048,1024]{1,0:T(8,128)(2,1)} %get-tuple-element.24, ...), custom_call_target="tpu_custom_call" | custom-call | tf_op jit(solution)/shard_map/collect/pallas_call | solution.py:1023

commit v4 on v3

--- a/solution.py
+++ b/solution.py
@@ -13,6 +13,9 @@
 TILE = 128
 RING = 4
 EPS = 1e-06
+EARLY = 4
+FORWARD = 5
+PASS = 3
 F32 = jnp.float32
 BF16 = jnp.bfloat16
 MESH = pl.DeviceIdType.MESH
@@ -337,16 +340,16 @@
         def _():
             step_c(s, c - 2)
 
-        @pl.when(c >= 3)
-        def _():
-            step_d(s, c - 3)
+        @pl.when(c >= FORWARD)
+        def _():
+            step_d(s, c - FORWARD)
 
     def late_tick(s, n):
         if n == 0:
             step_b(s, chunks - 1)
         if n <= 1:
             step_c(s, chunks - 2 + n)
-        step_d(s, chunks - 3 + n)
+        step_d(s, chunks - FORWARD + n)
 
     def gated_across(c):
         here = r.do.at[pl.ds(base(c), CHUNK), group_of(mp)]
@@ -375,14 +378,13 @@
         for t in range(width // 256):
             cols = pl.ds(t * 256, 256)
             total = dot_nn(r.do[rows, :], r.wof[:, cols])
-            r.own[0, :, cols] = total[:quarter]
-            r.own[1, :, cols] = total[quarter:]
+            r.branch[:, cols] = total
 
         def piece(i, carry):
             q, sub = i // 2, mult((i % 2) * 32, 32)
             held = pl.ds(mult(c * half + i * 32, 32), 32)
             full = pl.ds(mult(c * CHUNK + core * half + i * 32, 32), 32)
-            hidden = r.tok_half[held, :].astype(F32) + r.own[q, pl.ds(sub, 32), :]
+            hidden = r.tok_half[held, :].astype(F32) + r.branch[pl.ds(mult(i * 32, 32), 32), :]
             r.n2[full, :] = (hidden * rms_factor(hidden)).astype(BF16)
 
             @pl.when(q == side)
@@ -441,6 +443,107 @@
         rows = pl.ds(mult(tile * TILE, TILE), TILE)
         return tile, rows, lanes
 
+    def beside_copy(grads, arrivals, sems, g):
+        block = 2 * g + 1 - parity
+        send, recv = sems
+        return remote(
+            grads(pl.ds(mult(block * block_rows, block_rows), block_rows)),
+            arrivals(pl.ds(mult(g * block_rows, block_rows), block_rows)),
+            send.at[g],
+            recv.at[g],
+            beside,
+        )
+
+    def line_copy(grads, arrivals, sems, g):
+        block = 2 * g + parity
+        send, recv = sems
+        return remote(
+            grads(pl.ds(mult(block * block_rows, block_rows), block_rows)),
+            arrivals(line),
+            send.at[g],
+            recv.at[line],
+            (block, mp),
+        )
+
+    def glu_rows(rows):
+        return r.grad_g.at[:, rows]
+
+    def glu_beside(rows):
+        return r.xg_h.at[:, rows]
+
+    def glu_line(slot):
+        return r.zg_h.at[slot]
+
+    def att_rows(rows):
+        return r.d_right.at[:, rows, pl.ds(0, wide)]
+
+    def att_beside(rows):
+        return r.xa_h.at[:, rows]
+
+    def att_line(slot):
+        return r.za_h.at[slot]
+
+    glu_x = (glu_rows, glu_beside, (r.sem_xgs, r.sem_xgr))
+    glu_z = (glu_rows, glu_line, (r.sem_zgs, r.sem_zgr))
+    att_x = (att_rows, att_beside, (r.sem_xas, r.sem_xar))
+    att_z = (att_rows, att_line, (r.sem_zas, r.sem_zar))
+
+    def each(count, act):
+        def one(j, carry):
+            act(j)
+            return carry
+
+        if count == 1:
+            act(0)
+        else:
+            lax.fori_loop(0, count, one, 0)
+
+    def turn(k):
+        return (line // per_group + 1 + k) % groups
+
+    def turned_half(src, i, h):
+        for k in range(tokens // 512):
+            rows = pl.ds(h * (tokens // 2) + k * 256, 256)
+            r.turned[:, pl.ds(k * 256, 256)] = src[rows, pl.ds(mult(i * 256, 256), 256)].T
+
+    def gathered(h, old, term):
+        return (term if h == 0 else old.astype(F32) + term).astype(BF16)
+
+    def glu_half(i, h):
+        rows = pl.ds(mult(i * 256, 256), 256)
+        half_rows_all = pl.ds(h * (tokens // 2), tokens // 2)
+        turned_half(r.n2, i, h)
+        for t in range(fp // 256):
+            cols = pl.ds(t * 256, 256)
+            term = dot_nn(r.turned[...], r.d_left[half_rows_all, cols])
+            r.grad_g[0, rows, cols] = gathered(h, r.grad_g[0, rows, cols], term)
+            term = dot_nn(r.turned[...], r.d_right[h, :, cols])
+            r.grad_g[1, rows, cols] = gathered(h, r.grad_g[1, rows, cols], term)
+        turned_half(r.cot, i, h)
+        for t in range(fp // 256):
+            cols = pl.ds(t * 256, 256)
+            term = dot_nn(r.turned[...], r.mixed[half_rows_all, cols])
+            r.grad_g[2, rows, cols] = gathered(h, r.grad_g[2, rows, cols], term)
+
+    def att_half(i, h):
+        rows = pl.ds(mult(i * 256, 256), 256)
+        half_rows_all = pl.ds(h * (tokens // 2), tokens // 2)
+
+        def store(kind, term):
+            for u in range(wc // 128):
+                at_col = kind * (wc // 128) + u
+                cols = pl.ds((at_col % (wide // 128)) * 128, 128)
+                place = at_col // (wide // 128)
+                piece = term[:, u * 128 : u * 128 + 128]
+                r.d_right[place, rows, cols] = gathered(h, r.d_right[place, rows, cols], piece)
+
+        turned_half(r.n1, i, h)
+        for kind in range(4):
+            cols = pl.ds(kind * wc, wc)
+            store(kind, dot_nn(r.turned[...], r.d_all[half_rows_all, cols]))
+        turned_half(r.do, i, h)
+        store(4, dot_nn(r.turned[...], r.gated[half_rows_all, :]))
+
     for copy in w_loads:
         copy.wait()
 
@@ -485,16 +588,16 @@
         gated_across(c).start()
         gated_partner(c).start()
 
-        @pl.when(c == 1)
+        @pl.when(c == PASS - 1)
         def _():
             wo_across().wait_recv()
             wo_forward().start()
 
-        @pl.when(c >= 1)
-        def _():
-            gated_pass(c - 1)
-
-        @pl.when(c == 2)
+        @pl.when(c >= PASS)
+        def _():
+            gated_pass(c - PASS)
+
+        @pl.when(c == PASS + 1)
         def _():
             wo_load.wait()
             wo_partner().wait_recv()
@@ -502,9 +605,9 @@
             for copy in (wo_across(), wo_partner(), wo_forward()):
                 copy.wait_send()
 
-        @pl.when(c >= 2)
-        def _():
-            gated_project(c - 2)
+        @pl.when(c >= PASS + 1)
+        def _():
+            gated_project(c - PASS - 1)
 
         return carry
 
@@ -517,14 +620,13 @@
     cot_load.wait()
 
     def phase_two(c, carry):
-        @pl.when(c == 0)
-        def _():
-            gated_pass(chunks - 1)
-            gated_project(chunks - 2)
-
-        @pl.when(c == 1)
-        def _():
-            gated_project(chunks - 1)
+        @pl.when(c < PASS)
+        def _():
+            gated_pass(chunks - PASS + c)
+
+        @pl.when(c <= PASS)
+        def _():
+            gated_project(chunks - PASS - 1 + c)
 
         gated_end(c)
         rows_all = pl.ds(base(c), CHUNK)
@@ -553,6 +655,11 @@
         lax.fori_loop(0, width // 256, parts, 0, unroll=True)
         pair_copy(2, c).start()
         pair_copy(1, c).start()
+
+        @pl.when(c >= half_chunks)
+        def _():
+            glu_half(turn(c - half_chunks), 0)
+
         tick(2, c)
 
         @pl.when(c >= 1)
@@ -569,153 +676,81 @@
         across_copy(1, c).start()
         return carry
 
-    lax.fori_loop(0, chunks, send_glu, 0)
-
-    def transposed(src, i, dst):
-        def piece(k, carry):
-            rows = pl.ds(mult(k * 256, 256), 256)
-            tile = src[rows, pl.ds(mult(i * 256, 256), 256)].T
-            dst[k // 4, :, pl.ds(mult((k % 4) * 256, 256), 256)] = tile
-            return carry
-
-        lax.fori_loop(0, tokens // 256, piece, 0)
-
-    def grad_of(turned, right, cols):
-        total = None
-        for k in range(2):
-            rows = pl.ds(k * (tokens // 2), tokens // 2)
-            operand = right[k, :, cols] if len(right.shape) == 3 else right[rows, cols]
-            term = dot_nn(turned[k], operand)
-            total = term if total is None else total + term
-        return total.astype(BF16)
-
-    def beside_copy(grads, arrivals, sems, g):
-        block = 2 * g + 1 - parity
-        send, recv = sems
-        return remote(
-            grads(pl.ds(mult(block * block_rows, block_rows), block_rows)),
-            arrivals(pl.ds(mult(g * block_rows, block_rows), block_rows)),
-            send.at[g],
-            recv.at[g],
-            beside,
-        )
-
-    def line_copy(grads, arrivals, sems, g):
-        block = 2 * g + parity
-        send, recv = sems
-        return remote(
-            grads(pl.ds(mult(block * block_rows, block_rows), block_rows)),
-            arrivals(line),
-            send.at[g],
-            recv.at[line],
-            (block, mp),
-        )
-
-    def glu_rows(rows):
-        return r.grad_g.at[:, rows]
-
-    def glu_beside(rows):
-        return r.xg_h.at[:, rows]
-
-    def glu_line(slot):
-        return r.zg_h.at[slot]
-
-    def att_rows(rows):
-        return r.d_right.at[:, rows, pl.ds(0, wide)]
-
-    def att_beside(rows):
-        return r.xa_h.at[:, rows]
-
-    def att_line(slot):
-        return r.za_h.at[slot]
-
-    glu_x = (glu_rows, glu_beside, (r.sem_xgs, r.sem_xgr))
-    glu_z = (glu_rows, glu_line, (r.sem_zgs, r.sem_zgr))
-    att_x = (att_rows, att_beside, (r.sem_xas, r.sem_xar))
-    att_z = (att_rows, att_line, (r.sem_zas, r.sem_zar))
-
-    def each(count, act):
-        def one(j, carry):
-            act(j)
-            return carry
-
-        if count == 1:
-            act(0)
-        else:
-            lax.fori_loop(0, count, one, 0)
-
-    def glu_group(i, carry):
-        rows = pl.ds(mult(i * 256, 256), 256)
-        transposed(r.n2, i, r.part)
-
-        def sides(t, carry2):
-            cols = pl.ds(mult(t * 256, 256), 256)
-            r.grad_g[0, rows, cols] = grad_of(r.part, r.d_left, cols)
-            r.grad_g[1, rows, cols] = grad_of(r.part, r.d_right, cols)
-            return carry2
-
-        lax.fori_loop(0, fp // 256, sides, 0, unroll=True)
-        transposed(r.cot, i, r.part_g)
-
-        def down(t, carry2):
-            cols = pl.ds(mult(t * 256, 256), 256)
-            r.grad_g[2, rows, cols] = grad_of(r.part_g, r.mixed, cols)
-            return carry2
-
-        lax.fori_loop(0, fp // 256, down, 0, unroll=True)
+    lax.fori_loop(0, EARLY, send_glu, 0)
+
+    def glu_group(k, carry):
+        i = turn(k)
+        glu_half(i, 1)
         each(per_group, lambda j: beside_copy(*glu_x, i * per_group + j).start())
+        for n in range(FORWARD - 1):
+
+            @pl.when(k == n)
+            def _():
+                late_tick(2, n + 1)
+
         return carry
 
     lax.fori_loop(0, groups, glu_group, 0)
 
-    def line_step(kinds, lanes, x, z, arrivals_h, stage, grads, g):
-        copy = beside_copy(*x, g)
-        copy.wait_recv()
-        copy.wait_send()
+    def line_loads(kinds, lanes, arrivals_h, stage, g):
         here = pl.ds(mult(g * block_rows, block_rows), block_rows)
-        loads = []
-        for t in range(kinds):
-            load = pltpu.make_async_copy(
+        return [
+            pltpu.make_async_copy(
                 arrivals_h.at[t, here],
                 stage.at[pl.ds(t * block_rows, block_rows), pl.ds(0, lanes)],
                 r.sem_stage.at[t],
             )
+            for t in range(kinds)
+        ]
+
+    def line_arrive(kinds, lanes, x, z, arrivals_h, stage, grads, g):
+        copy = beside_copy(*x, g)
+        copy.wait_recv()
+        copy.wait_send()
+        for load in line_loads(kinds, lanes, arrivals_h, stage, g):
             load.start()
-            loads.append(load)
-        for load in loads:
+
+    def line_sum(kinds, lanes, x, z, arrivals_h, stage, grads, g):
+        for load in line_loads(kinds, lanes, arrivals_h, stage, g):
             load.wait()
         step = min(16, block_rows)
         cols = pl.ds(0, lanes)
 
-        for t in range(kinds):
-
-            def piece(i, carry):
-                sub = mult(i * step, step)
-                there = pl.ds(mult((2 * g + parity) * block_rows + sub, step), step)
+        def piece(i, carry):
+            sub = mult(i * step, step)
+            there = pl.ds(mult((2 * g + parity) * block_rows + sub, step), step)
+            for t in range(kinds):
                 mine = grads[t, there, cols].astype(F32)
                 theirs = stage[pl.ds(mult(t * block_rows + sub, step), step), cols].astype(F32)
                 grads[t, there, cols] = (mine + theirs).astype(BF16)
-                return carry
-
-            lax.fori_loop(0, block_rows // step, piece, 0)
+            return carry
+
+        lax.fori_loop(0, block_rows // step, piece, 0)
 
         @pl.when(g != line)
         def _():
             line_copy(*z, g).start()
 
-    def glu_line_step(g):
-        line_step(3, fp, glu_x, glu_z, r.xg_h, r.mixed, r.grad_g, g)
-
-    def att_line_step(g):
-        line_step(2, wide, att_x, att_z, r.xa_h, r.d_left, r.d_right, g)
+    glu_line = (3, fp, glu_x, glu_z, r.xg_h, r.mixed, r.grad_g)
+    att_line_of = (2, wide, att_x, att_z, r.xa_h, r.d_left, r.d_right)
+
+    def line_both(what, k):
+        if per_group == 1:
+            line_sum(*what, turn(k))
+            return
+
+        def one(j):
+            g = turn(k) * per_group + j
+            line_arrive(*what, g)
+            line_sum(*what, g)
+
+        each(per_group, one)
+
+    def line_start(what, k):
+        if per_group == 1:
+            line_arrive(*what, turn(k))
 
     def phase_three(c, carry):
-        for n in range(2):
-
-            @pl.when(c == n)
-            def _():
-                late_tick(2, n + 1)
-
         step_e(2, c)
         rows_all = pl.ds(base(c), CHUNK)
         r.gate_now[...] = dot_nt(r.do[rows_all, :], r.wof[group_of(mp), :])
@@ -756,40 +791,40 @@
 
         lax.fori_loop(0, width // 256, back_piece, 0, unroll=True)
         pair_copy(3, c).start()
+
+        @pl.when(c >= half_chunks)
+        def _():
+            att_half(turn(c - half_chunks), 0)
+
         tick(3, c)
 
         for i in range(groups):
 
             @pl.when(c == 2 * i + 1)
             def _():
-                each(per_group, lambda j: glu_line_step(i * per_group + j))
+                line_start(glu_line, i)
+
+            if i > 0:
+
+                @pl.when(c == 2 * i)
+                def _():
+                    line_both(glu_line, i - 1)
 
         return carry
 
     lax.fori_loop(0, chunks, phase_three, 0)
     late_tick(3, 0)
 
-    def att_group(i, carry):
-        rows = pl.ds(mult(i * 256, 256), 256)
-        transposed(r.n1, i, r.part_g)
-
-        def store(t, total):
-            for u in range(wc // 128):
-                at_col = t * (wc // 128) + u
-                cols = pl.ds(mult((at_col % (wide // 128)) * 128, 128), 128)
-                r.d_right[at_col // (wide // 128), rows, cols] = total[:, u * 128 : u * 128 + 128]
-
-        def four(t, carry2):
-            store(t, grad_of(r.part_g, r.d_all, pl.ds(mult(t * wc, wc), wc)))
-            return carry2
-
-        lax.fori_loop(0, 4, four, 0, unroll=True)
-        transposed(r.do, i, r.part_g)
-        store(4, grad_of(r.part_g, r.gated, pl.ds(0, wc)))
+    line_both(glu_line, groups - 1)
+    lax.fori_loop(EARLY, chunks, send_glu, 0)
+
+    def att_group(k, carry):
+        i = turn(k)
+        att_half(i, 1)
         each(per_group, lambda j: beside_copy(*att_x, i * per_group + j).start())
-        for n in range(2):
-
-            @pl.when(i == n)
+        for n in range(FORWARD - 1):
+
+            @pl.when(k == n)
             def _():
                 late_tick(3, n + 1)
 
@@ -801,13 +836,17 @@
         step_c(1, c)
         return carry
 
-    lax.fori_loop(0, chunks, glu_result, 0)
-
-    def att_lines(g, carry):
-        att_line_step(g)
+    lax.fori_loop(0, EARLY, glu_result, 0)
+
+    def att_lines(k, carry):
+        line_start(att_line_of, k)
+        first_left = EARLY + k * (chunks - EARLY) // groups
+        last_left = EARLY + (k + 1) * (chunks - EARLY) // groups
+        lax.fori_loop(first_left, last_left, glu_result, 0)
+        line_both(att_line_of, k)
         return carry
 
-    lax.fori_loop(0, pairs, att_lines, 0)
+    lax.fori_loop(0, groups, att_lines, 0)
 
     def glu_forward(c, carry):
         step_d(1, c)
@@ -899,6 +938,7 @@
         ("d_left", pltpu.VMEM((rows, fp), BF16)),
         ("d_right", pltpu.VMEM((2, rows // 2, fp), BF16)),
         ("do", pltpu.VMEM((rows, width), BF16)),
+        ("turned", pltpu.VMEM((256, rows // 2), BF16)),
         ("part", pltpu.VMEM((2, CHUNK, width), BF16)),
         ("part_g", pltpu.VMEM((2, CHUNK, width), BF16)),
         ("pair", pltpu.VMEM((RING, CHUNK // 2, width), BF16)),
@@ -908,6 +948,7 @@
         ("got", pltpu.VMEM((own, width), BF16)),
         ("got_g", pltpu.VMEM((own, width), BF16)),
         ("own", pltpu.VMEM((2, quarter, width), F32)),
+        ("branch", pltpu.VMEM((CHUNK // 2, width), F32)),
         ("own_g", pltpu.VMEM((own, width), BF16)),
         ("hidden", pltpu.VMEM((own, width), F32)),
         ("d_hidden", pltpu.VMEM((own, width), F32)),

time: 239 us -> 211 us (0.88); the launches traced: 235 us -> 211 us
  Pallas kernels: 234 us -> 210 us
    pallas_call x1, Pallas kernels: 225 us -> 201 us  [fused(): pl.pallas_call(call, out_shape=[jax.ShapeDtypeStruct(s, d) for _, s, d, _...]
where the time goes in v4:
time: 211 us
  Pallas kernels  210 us (100%)
    pallas_call x1, Pallas kernels, fused(): pl.pallas_call(call, out_shape=[jax.ShapeDtypeStruct(s, d) for _, s, d, _...  201 us
    pallas_call x1, Pallas kernels, collected(): pl.pallas_call(lambda *refs: collect(br, wc, ff, refs), out_shape=[jax.Sh...  8.55 us

profile of v4, /device:TPU:9, one launch (start us, length us, event | category | flops | bytes accessed | tf_op | source)
XLA Modules:
  0.0 210.7 jit_solution(882108922848951399)
XLA Ops:
  0.6 201.3 %fused_layer.1 = (bf16[2048,1024]{1,0:T(8,128)(2,1)}, bf16[2048,1024]{1,0:T(8,128)(2,1)}, bf16[3,512,768]{2,1,0:T(8,128)(2,1)}, bf16[2,512,640]{2,1,0:T(8,128)(2...) custom-call(bf16[2048,1024]{1,0:T(8,128)(2,1)} %refs_0_.1, s32[16,128]{1,0:T(8,128)} %bitcast.9, ...), custom_call_target="tpu_custom_call" | custom-call | flops 42681237504 | bytes 33554432 | tf_op jit(solution)/shard_map/fused_layer/pallas_call | solution.py:975
  201.9 8.6 %collect.1 = (bf16[2048,1024]{1,0:T(8,128)(2,1)}, bf16[2048,1024]{1,0:T(8,128)(2,1)}, f32[128,256]{1,0:T(8,128)}, f32[128,256]{1,0:T(8,128)}, f32[128,256]{1,0:T...) custom-call(bf16[2048,1024]{1,0:T(8,128)(2,1)} %get-tuple-element.24, ...), custom_call_target="tpu_custom_call" | custom-call | tf_op jit(solution)/shard_map/collect/pallas_call | solution.py:1064

commit v5 on v4

--- a/solution.py
+++ b/solution.py
@@ -15,7 +15,7 @@
 EPS = 1e-06
 EARLY = 4
 FORWARD = 5
-PASS = 3
+PASS = 6
 F32 = jnp.float32
 BF16 = jnp.bfloat16
 MESH = pl.DeviceIdType.MESH
@@ -86,19 +86,20 @@
         )
 
     barrier = pltpu.get_barrier_semaphore()
-    for device in (partner, across, beside):
+    for device in (partner, across):
         pl.semaphore_signal(barrier, inc=1, device_id=device, device_id_type=MESH)
+    near = min(8, ndp)
+    near_at = dp % near
+    near_base = dp - near_at
 
     def greet(j, carry):
-        @pl.when(j != line)
-        def _():
-            pl.semaphore_signal(
-                barrier, inc=1, device_id=(2 * j + parity, mp), device_id_type=MESH
-            )
+        @pl.when((j != dp) & ((j % 2 == parity) | (j // near == dp // near)))
+        def _():
+            pl.semaphore_signal(barrier, inc=1, device_id=(j, mp), device_id_type=MESH)
 
         return carry
 
-    lax.fori_loop(0, pairs, greet, 0)
+    lax.fori_loop(0, ndp, greet, 0)
 
     pair_mp = mp + 1 - 2 * core
     across_mp = mp + 2 - 4 * side
@@ -106,9 +107,39 @@
     def group_of(who):
         return pl.ds(mult(who * wc, wc), wc)
 
+    share = wc // near
+
+    def share_of(who, place):
+        return pl.ds(mult(who * wc + place * share, share), share)
+
     def wo_across():
-        there = r.wof.at[group_of(mp)]
-        return remote(r.wo_h, there, r.sem_wos.at[0], r.sem_wor.at[0], across)
+        return remote(
+            r.wo_h.at[pl.ds(mult(near_at * share, share), share)],
+            r.wof.at[share_of(mp, near_at)],
+            r.sem_wos.at[0],
+            r.sem_wor.at[0],
+            across,
+        )
+
+    def wo_spread(j):
+        here = r.wof.at[share_of(across_mp, near_at)]
+        return remote(
+            here, here, r.sem_wos.at[3 + j], r.sem_wor.at[3 + near_at], (near_base + j, mp)
+        )
+
+    def wo_arrival(j):
+        here = r.wof.at[share_of(across_mp, j)]
+        return remote(here, here, r.sem_wos.at[3 + j], r.sem_wor.at[3 + j], (near_base + j, mp))
+
+    def to_near(act):
+        def one(j, carry):
+            @pl.when(j != near_at)
+            def _():
+                act(j)
+
+            return carry
+
+        lax.fori_loop(0, near, one, 0)
 
     def wo_partner():
         there = r.wof.at[group_of(mp)]
@@ -144,7 +175,7 @@
     cot_load = pltpu.make_async_copy(r.cot_h, r.cot, r.sem_w.at[8])
     cot_load.start()
 
-    pl.semaphore_wait(barrier, 3 + pairs - 1)
+    pl.semaphore_wait(barrier, 2 + pairs - 1 + near // 2)
     for copy in (wo_across(), wo_partner()):
         copy.start()
 
@@ -558,7 +589,7 @@
             r.n1[rows, :] = (x * rms_factor(x)).astype(BF16)
             return carry2
 
-        lax.fori_loop(0, CHUNK // 32, norm_piece, 0)
+        lax.fori_loop(0, CHUNK // 32, norm_piece, 0, unroll=True)
 
         def project(t, carry2):
             cols = pl.ds(mult(t * wc, wc), wc)
@@ -588,9 +619,14 @@
         gated_across(c).start()
         gated_partner(c).start()
 
-        @pl.when(c == PASS - 1)
+        @pl.when(c == 0)
         def _():
             wo_across().wait_recv()
+            to_near(lambda j: wo_spread(j).start())
+
+        @pl.when(c == PASS)
+        def _():
+            to_near(lambda j: wo_arrival(j).wait_recv())
             wo_forward().start()
 
         @pl.when(c >= PASS)
@@ -604,6 +640,7 @@
             wo_forward().wait_recv()
             for copy in (wo_across(), wo_partner(), wo_forward()):
                 copy.wait_send()
+            to_near(lambda j: wo_spread(j).wait_send())
 
         @pl.when(c >= PASS + 1)
         def _():
@@ -959,8 +996,8 @@
     ]
     for name in ("as", "ar", "bs", "br", "cs", "cr", "ps", "pr", "ds", "dr"):
         scratch.append(("sem_" + name, dma((4 * chunks,))))
-    scratch.append(("sem_wos", dma((3,))))
-    scratch.append(("sem_wor", dma((3,))))
+    scratch.append(("sem_wos", dma((11,))))
+    scratch.append(("sem_wor", dma((11,))))
     scratch.append(("sem_o", dma((2 * chunks,))))
     for name in ("xgs", "xgr", "zgs", "zgr", "xas", "xar", "zas", "zar"):
         scratch.append(("sem_" + name, dma((pairs,))))

time: 211 us -> 202 us (0.957)
  Pallas kernels: 210 us -> 201 us
    pallas_call x1, Pallas kernels: 201 us -> 193 us  [fused(): pl.pallas_call(call, out_shape=[jax.ShapeDtypeStruct(s, d) for _, s, d, _...]
where the time goes in v5:
time: 202 us
  Pallas kernels  201 us (100%)
    pallas_call x1, Pallas kernels, fused(): pl.pallas_call(call, out_shape=[jax.ShapeDtypeStruct(s, d) for _, s, d, _...  193 us
    pallas_call x1, Pallas kernels, collected(): pl.pallas_call(lambda *refs: collect(br, wc, ff, refs), out_shape=[jax.Sh...  8.55 us

profile of v5, /device:TPU:9, one launch (start us, length us, event | category | flops | bytes accessed | tf_op | source)
XLA Modules:
  0.0 202.2 jit_solution(9458685173975005432)
XLA Ops:
  0.6 192.9 %fused_layer.1 = (bf16[2048,1024]{1,0:T(8,128)(2,1)}, bf16[2048,1024]{1,0:T(8,128)(2,1)}, bf16[3,512,768]{2,1,0:T(8,128)(2,1)}, bf16[2,512,640]{2,1,0:T(8,128)(2...) custom-call(bf16[2048,1024]{1,0:T(8,128)(2,1)} %refs_0_.1, s32[16,128]{1,0:T(8,128)} %bitcast.9, ...), custom_call_target="tpu_custom_call" | custom-call | flops 42681237504 | bytes 33554432 | tf_op jit(solution)/shard_map/fused_layer/pallas_call | solution.py:1012
  193.5 8.6 %collect.1 = (bf16[2048,1024]{1,0:T(8,128)(2,1)}, bf16[2048,1024]{1,0:T(8,128)(2,1)}, f32[128,256]{1,0:T(8,128)}, f32[128,256]{1,0:T(8,128)}, f32[128,256]{1,0:T...) custom-call(bf16[2048,1024]{1,0:T(8,128)(2,1)} %get-tuple-element.24, ...), custom_call_target="tpu_custom_call" | custom-call | tf_op jit(solution)/shard_map/collect/pallas_call | solution.py:1101

commit v6 on v5

--- a/solution.py
+++ b/solution.py
@@ -15,7 +15,8 @@
 EPS = 1e-06
 EARLY = 4
 FORWARD = 5
-PASS = 6
+PASS = 5
+SKEW = 7
 F32 = jnp.float32
 BF16 = jnp.bfloat16
 MESH = pl.DeviceIdType.MESH
@@ -463,7 +464,7 @@
         top = jnp.max(masked, axis=-1, keepdims=True)
         expd = jnp.exp(masked - top)
         probs = expd * (1.0 / jnp.sum(expd, axis=-1, keepdims=True))
-        return probs, stack, keys
+        return probs
 
     head_pairs = wc // TILE
     tiles = CHUNK // TILE
@@ -575,10 +576,16 @@
         turned_half(r.do, i, h)
         store(4, dot_nn(r.turned[...], r.gated[half_rows_all, :]))
 
+    def probs_out(c):
+        return pltpu.make_async_copy(r.probs.at[c % 2], r.probs_h.at[c], r.sem_po.at[c % 2])
+
+    def probs_in(c):
+        return pltpu.make_async_copy(r.probs_h.at[c], r.probs.at[c % 2], r.sem_pi.at[c % 2])
+
     for copy in w_loads:
         copy.wait()
 
-    def phase_one(c, carry):
+    def phase_one(c):
         rows_all = pl.ds(base(c), CHUNK)
         load_tokens(c).wait()
         r.tok_half[pl.ds(mult(c * half, half), half), :] = r.n1[half_rows(c), :]
@@ -600,11 +607,16 @@
         r.gate_now[...] = dot_nn(r.n1[rows_all, :], r.w[:, pl.ds(3 * wc, wc)])
         r.gate[rows_all, :] = r.gate_now[...].astype(BF16)
 
+        @pl.when(c >= 2)
+        def _():
+            probs_out(c - 2).wait()
+
         def attend(i, carry2):
             tile, rows, lanes = tile_of(c, i)
-            probs, _, _ = probs_of(tile, rows, lanes)
+            probs = probs_of(tile, rows, lanes).astype(BF16)
+            r.probs[c % 2, i] = probs
             values = r.qkv[rows, pl.ds(2 * wc + lanes, TILE)]
-            attended = unstacked(dot_nn(probs.astype(BF16), values))
+            attended = unstacked(dot_nn(probs, values))
             r.attended[rows, pl.ds(lanes, TILE)] = attended.astype(BF16)
             factor = lax.rsqrt(head_mean(attended * attended) + EPS)
             near = pl.ds(mult((i // head_pairs) * TILE, TILE), TILE)
@@ -616,55 +628,11 @@
 
         lax.fori_loop(0, tiles * head_pairs, attend, 0, unroll=True)
 
+        probs_out(c).start()
         gated_across(c).start()
         gated_partner(c).start()
 
-        @pl.when(c == 0)
-        def _():
-            wo_across().wait_recv()
-            to_near(lambda j: wo_spread(j).start())
-
-        @pl.when(c == PASS)
-        def _():
-            to_near(lambda j: wo_arrival(j).wait_recv())
-            wo_forward().start()
-
-        @pl.when(c >= PASS)
-        def _():
-            gated_pass(c - PASS)
-
-        @pl.when(c == PASS + 1)
-        def _():
-            wo_load.wait()
-            wo_partner().wait_recv()
-            wo_forward().wait_recv()
-            for copy in (wo_across(), wo_partner(), wo_forward()):
-                copy.wait_send()
-            to_near(lambda j: wo_spread(j).wait_send())
-
-        @pl.when(c >= PASS + 1)
-        def _():
-            gated_project(c - PASS - 1)
-
-        return carry
-
-    lax.fori_loop(0, chunks, phase_one, 0)
-
-    for copy in glu_loads:
-        copy.wait()
-    for weights in (r.wd, r.wl, r.wr):
-        weights[pl.ds(ff, fp - ff), :] = jnp.zeros((fp - ff, width), BF16)
-    cot_load.wait()
-
-    def phase_two(c, carry):
-        @pl.when(c < PASS)
-        def _():
-            gated_pass(chunks - PASS + c)
-
-        @pl.when(c <= PASS)
-        def _():
-            gated_project(chunks - PASS - 1 + c)
-
+    def phase_two(c):
         gated_end(c)
         rows_all = pl.ds(base(c), CHUNK)
         rows_half = pl.ds(mult((c % half_chunks) * CHUNK, CHUNK), CHUNK)
@@ -703,9 +671,53 @@
         def _():
             step_b(1, c - 1, send=False)
 
+    def both(it, carry):
+        @pl.when(it < chunks)
+        def _():
+            phase_one(it)
+
+        @pl.when(it == 0)
+        def _():
+            wo_across().wait_recv()
+            to_near(lambda j: wo_spread(j).start())
+
+        @pl.when(it == PASS)
+        def _():
+            to_near(lambda j: wo_arrival(j).wait_recv())
+            wo_forward().start()
+
+        @pl.when((it >= PASS) & (it < chunks + PASS))
+        def _():
+            gated_pass(it - PASS)
+
+        @pl.when(it == PASS + 1)
+        def _():
+            wo_load.wait()
+            wo_partner().wait_recv()
+            wo_forward().wait_recv()
+            for copy in (wo_across(), wo_partner(), wo_forward()):
+                copy.wait_send()
+            to_near(lambda j: wo_spread(j).wait_send())
+            for copy in glu_loads:
+                copy.wait()
+            for weights in (r.wd, r.wl, r.wr):
+                weights[pl.ds(ff, fp - ff), :] = jnp.zeros((fp - ff, width), BF16)
+            cot_load.wait()
+
+        @pl.when((it >= PASS + 1) & (it < chunks + PASS + 1))
+        def _():
+            gated_project(it - PASS - 1)
+
+        @pl.when(it >= SKEW)
+        def _():
+            phase_two(it - SKEW)
+
         return carry
 
-    lax.fori_loop(0, chunks, phase_two, 0)
+    lax.fori_loop(0, chunks + SKEW, both, 0)
+    for c in range(chunks - 2, chunks):
+        probs_out(c).wait()
+    probs_in(0).start()
     late_tick(2, 0)
     step_b(1, chunks - 1, send=False)
 
@@ -788,6 +800,12 @@
             line_arrive(*what, turn(k))
 
     def phase_three(c, carry):
+        probs_in(c).wait()
+
+        @pl.when(c + 1 < chunks)
+        def _():
+            probs_in(c + 1).start()
+
         step_e(2, c)
         rows_all = pl.ds(base(c), CHUNK)
         r.gate_now[...] = dot_nt(r.do[rows_all, :], r.wof[group_of(mp), :])
@@ -806,10 +824,13 @@
             r.d_all[rows, pl.ds(3 * wc + lanes, TILE)] = d_gate.astype(BF16)
             d_att = factor * (d_head - head_normed * head_mean(d_head * head_normed))
             d_stack = stacked(d_att.astype(BF16))
-            probs, stack, keys = probs_of(tile, rows, lanes)
+            probs_low = r.probs[c % 2, i]
+            probs = probs_low.astype(F32)
+            stack = stacked(r.qkv[rows, here])
+            keys = r.qkv[rows, pl.ds(wc + lanes, TILE)]
             values = r.qkv[rows, pl.ds(2 * wc + lanes, TILE)]
             d_probs = dot_nt(d_stack, values)
-            d_values = dot_tn(probs.astype(BF16), d_stack)
+            d_values = dot_tn(probs_low, d_stack)
             r.d_all[rows, pl.ds(2 * wc + lanes, TILE)] = d_values.astype(BF16)
             delta = jnp.sum(probs * d_probs, axis=-1, keepdims=True)
             d_scores = (probs * (d_probs - delta)).astype(BF16)
@@ -932,6 +953,7 @@
     br = width // ndp
     pairs = ndp // 2
     wide = 5 * wc // 2
+    probs_shape = (CHUNK // TILE * wc // TILE, 2 * TILE, TILE)
     hbm = pl.BlockSpec(memory_space=pl.ANY)
     vmem = pl.BlockSpec(memory_space=pltpu.VMEM)
     ins = [
@@ -954,6 +976,7 @@
         ("xa_h", (2, pairs * br, wide), BF16, hbm),
         ("zg_h", (pairs, 3, br, fp), BF16, hbm),
         ("za_h", (pairs, 2, br, wide), BF16, hbm),
+        ("probs_h", (chunks,) + probs_shape, BF16, hbm),
     ]
     dma = pltpu.SemaphoreType.DMA
     scratch = [
@@ -990,6 +1013,9 @@
         ("hidden", pltpu.VMEM((own, width), F32)),
         ("d_hidden", pltpu.VMEM((own, width), F32)),
         ("grad_g", pltpu.VMEM((3, width, fp), BF16)),
+        ("probs", pltpu.VMEM((2,) + probs_shape, BF16)),
+        ("sem_po", dma((2,))),
+        ("sem_pi", dma((2,))),
         ("sem_tok", dma((chunks,))),
         ("sem_w", dma((9,))),
         ("sem_stage", dma((3 * pairs,))),

time: 202 us -> 199 us (0.985)
  Pallas kernels: 201 us -> 198 us
    pallas_call x1, Pallas kernels: 193 us -> 190 us  [fused(): pl.pallas_call(call, out_shape=[jax.ShapeDtypeStruct(s, d) for _, s, d, _...]
where the time goes in v6:
time: 199 us
  Pallas kernels  198 us (99%)
    pallas_call x1, Pallas kernels, fused(): pl.pallas_call(call, out_shape=[jax.ShapeDtypeStruct(s, d) for _, s, d, _...  190 us
    pallas_call x1, Pallas kernels, collected(): pl.pallas_call(lambda *refs: collect(br, wc, ff, refs), out_shape=[jax.Sh...  8.55 us

profile of v6, /device:TPU:9, one launch (start us, length us, event | category | flops | bytes accessed | tf_op | source)
XLA Modules:
  0.0 199.2 jit_solution(10845357627303838507)
XLA Ops:
  0.6 189.8 %fused_layer.1 = (bf16[2048,1024]{1,0:T(8,128)(2,1)}, bf16[2048,1024]{1,0:T(8,128)(2,1)}, bf16[3,512,768]{2,1,0:T(8,128)(2,1)}, bf16[2,512,640]{2,1,0:T(8,128)(2...) custom-call(bf16[2048,1024]{1,0:T(8,128)(2,1)} %refs_0_.1, ...), custom_call_target="tpu_custom_call" | custom-call | flops 42681237504 | bytes 33554432 | tf_op jit(solution)/shard_map/fused_layer/pallas_call | solution.py:1038
  190.5 8.6 %collect.1 = (bf16[2048,1024]{1,0:T(8,128)(2,1)}, bf16[2048,1024]{1,0:T(8,128)(2,1)}, f32[128,256]{1,0:T(8,128)}, f32[128,256]{1,0:T(8,128)}, f32[128,256]{1,0:T...) custom-call(bf16[2048,1024]{1,0:T(8,128)(2,1)} %get-tuple-element.24, ...), custom_call_target="tpu_custom_call" | custom-call | tf_op jit(solution)/shard_map/collect/pallas_call | solution.py:1127
